TPU v7x, 32 devices: a whole 2x2x4 slice. The times are simulated.
32 devices in a mesh: train: 4 (over z), serve: 8 (over y, x, core).
Axes of the slice: x: 2, y: 2, z: 4, core: 2. Of those that a mesh axis runs over, the one named last changes fastest.
Arguments:
- train_weights: bfloat16 [16, 7424, 2112], P(None, 'train', 'serve'), may hold values from -6 to 6
- row_offset: int32 [16, 5], replicated, may hold values from 0 to 7168, as said below
- block_group: int32 [16, 224, 1], P(None, 'train'), may hold values from 0 to 7; in each aligned block of 56 rows (0 to 55, 56 to 111, ..., all dimensions but the last counted through in order) at most 8 rows name the same one
Outputs:
- quant_codes: bfloat16 [16, 8, 4, 8, 32, 2112], P(None, 'serve', 'train')
- block_scales: float32 [16, 8, 4, 8, 2112], P(None, 'serve', 'train')
Inputs may be any that keep to these rules, and one draw needn't show every extreme that they name: For every layer l: row_offset[l, 0] = 0 and row_offset[l, 4] = 7168; every other row_offset[l, t] lies 1 to 32 rows above or below t * 1792, never on it; in every layer one entry lies exactly 32 rows above and another exactly 32 rows below; layer 1 has the opposite sign of layer 0 at every such entry. `block_group`: within each aligned block of 56 entries (one training device's blocks of one layer), no group is named more than 8 times; some group reaches 8 in some of them.
All inputs are finite; a program needn't handle non-finite values.
Results may differ from a plain program's by a relative error of at most 0.001.
Values may be sent and summed in bfloat16 or wider, within the bound.
A program may use at most 128 MiB of HBM per device.

v0:
```python
import functools

import jax
import jax.numpy as jnp
from jax import lax
from jax.experimental import pallas as pl
from jax.experimental.pallas import tpu as pltpu
from jax.sharding import PartitionSpec as P

BLOCK = 32
SHIFT = 32
LANES = 128
PAIR = 2


def turned(values):
    return jnp.transpose(values.astype(jnp.float32))


def pack_kernel(base, slots_n, group_ref, order_ref, first_ref, next_ref, wt_ref, left_ref, right_ref, *refs):
    out_ref, rem_ref, w_ref = refs[-3:]
    step = pl.program_id(0)
    columns, buffer_len = wt_ref.shape[1:]
    full = columns // LANES
    rem = columns - full * LANES
    blocks_dev = group_ref.shape[1]
    groups = out_ref.shape[0]
    row = lax.broadcasted_iota(jnp.int32, (BLOCK, columns), 0)
    for sub in range(PAIR):
        layer = (base + step) * PAIR + sub
        for low in range(0, buffer_len, LANES):
            high = min(low + LANES, buffer_len)
            w_ref[sub, low:high, :] = turned(wt_ref[sub, :, low:high]).astype(w_ref.dtype)

        def place(j, block, sub=sub, layer=layer):
            g = group_ref[layer, j]
            k = order_ref[layer, j]
            for t in range(full):
                out_ref[g, 0, (sub * slots_n + k) * full + t] = block[:, t * LANES : (t + 1) * LANES]
            if rem:
                rem_ref[g, sub * slots_n + k, :, 0:rem] = block[:, full * LANES :]

        def inner(j, carry, sub=sub, place=place):
            start = pl.multiple_of(SHIFT + j * BLOCK, BLOCK)
            place(j, w_ref[sub, pl.ds(start, BLOCK), :])
            return carry

        lax.fori_loop(1, blocks_dev - 1, inner, 0, unroll=6 if (blocks_dev - 2) % 6 == 0 else 2)
        head = jnp.where(
            row < first_ref[layer],
            left_ref[sub].astype(jnp.float32),
            w_ref[sub, SHIFT : SHIFT + BLOCK, :].astype(jnp.float32),
        )
        place(0, head.astype(out_ref.dtype))
        last = (blocks_dev - 1) * BLOCK
        tail = jnp.where(
            row + last >= next_ref[layer],
            right_ref[sub].astype(jnp.float32),
            w_ref[sub, SHIFT + last : SHIFT + last + BLOCK, :].astype(jnp.float32),
        )
        place(blocks_dev - 1, tail.astype(out_ref.dtype))
    if rem:
        lane = lax.broadcasted_iota(jnp.int32, (BLOCK, LANES), 1)

        def gather(g, carry):
            tile = rem_ref[g, 0].astype(jnp.float32)
            for i in range(1, PAIR * slots_n):
                moved = pltpu.roll(rem_ref[g, i].astype(jnp.float32), i * rem, 1)
                tile = jnp.where(lane >= i * rem, moved, tile)
            out_ref[g, 0, PAIR * slots_n * full] = tile.astype(out_ref.dtype)
            return carry

        lax.fori_loop(0, groups, gather, 0)


def unpack_kernel(base, slots_n, columns, count_ref, *refs):
    recv_ref, codes_ref, scale_ref, rem_code, rem_scale = refs[0], *refs[-4:]
    step = pl.program_id(0)
    full = columns // LANES
    rem = columns - full * LANES
    sources = recv_ref.shape[0]
    width = codes_ref.shape[3]
    tiles = -(-width // LANES)

    def scaled(values):
        values = values.astype(jnp.float32)
        divisor = jnp.maximum(jnp.max(jnp.abs(values), axis=0, keepdims=True), 0.25)
        return values * (1.0 / divisor), divisor

    if rem:
        for s in range(sources):
            rem_code[s], rem_scale[s] = scaled(recv_ref[s, 0, PAIR * slots_n * full])
    lane = lax.broadcasted_iota(jnp.int32, (BLOCK, LANES), 1)
    lane_row = lax.broadcasted_iota(jnp.int32, (1, LANES), 1)

    for sub in range(PAIR):
        count = count_ref[(base + step) * PAIR + sub]
        for k in range(slots_n):
            i = sub * slots_n + k

            @pl.when(k < count)
            def _():
                parts = [None] * tiles

                def put(tile, low, code, scale):
                    if tile >= tiles:
                        return
                    if parts[tile] is None:
                        parts[tile] = (code, scale)
                    else:
                        before = parts[tile]
                        parts[tile] = (
                            jnp.where(lane >= low, code, before[0]),
                            jnp.where(lane_row >= low, scale, before[1]),
                        )

                def flush(below):
                    for tile in range(below):
                        if parts[tile] is not None:
                            code, scale = parts[tile]
                            end = min(width, (tile + 1) * LANES)
                            size = end - tile * LANES
                            codes_ref[sub, k, :, tile * LANES : end] = code[:, :size].astype(codes_ref.dtype)
                            scale_ref[sub, k : k + 1, tile * LANES : end] = scale[:, :size]
                            parts[tile] = None

                for s in range(sources):
                    for t in range(full + (1 if rem else 0)):
                        start = s * columns + t * LANES
                        size = LANES if t < full else rem
                        low = start % LANES
                        if t < full:
                            code, scale = scaled(recv_ref[s, 0, i * full + t])
                            turn = low
                        else:
                            code, scale = rem_code[s], rem_scale[s]
                            turn = (low - i * rem) % LANES
                        if turn:
                            code = pltpu.roll(code, turn, 1)
                            scale = pltpu.roll(scale, turn, 1)
                        tile = start // LANES
                        put(tile, low, code, scale)
                        if low + size > LANES:
                            put(tile + 1, 0, code, scale)
                        flush((start + size) // LANES)
                flush(tiles)

            @pl.when(k >= count)
            def _():
                codes_ref[sub, k] = jnp.zeros((BLOCK, width), codes_ref.dtype)
                scale_ref[sub, k : k + 1] = jnp.zeros((1, width), scale_ref.dtype)


def shards(train_weights, row_offset, block_group):
    train_n = lax.axis_size("train")
    serve_n = lax.axis_size("serve")
    train_idx = lax.axis_index("train")
    serve_idx = lax.axis_index("serve")
    layers, buffer_len, columns = train_weights.shape
    rows_dev = buffer_len - 2 * SHIFT
    blocks_dev = block_group.shape[1]
    slots_n = (blocks_dev + serve_n - 1) // serve_n + 1
    full = columns // LANES
    rem = columns - full * LANES
    assert PAIR * slots_n * rem <= LANES and layers % PAIR == 0
    pieces = PAIR * slots_n * full + (1 if rem else 0)
    pairs = layers // PAIR
    ends = [max(1, pairs // 4), max(1, pairs // 8)]
    sizes = [ends[0], pairs - sum(ends), ends[1]] if pairs > sum(ends) else [pairs]
    firsts = [sum(sizes[:c]) for c in range(len(sizes))]
    width = columns * serve_n
    dtype = train_weights.dtype

    entries = jnp.arange(train_n + 1, dtype=jnp.int32)
    position = jnp.arange(blocks_dev, dtype=jnp.int32)
    earlier = position[None, :] < position[:, None]
    group_ids = block_group[:, :, 0]
    first_row = jnp.sum(jnp.where(entries[None, :] == train_idx, row_offset, 0), axis=1) - train_idx * rows_dev
    next_row = jnp.sum(jnp.where(entries[None, :] == train_idx + 1, row_offset, 0), axis=1) - train_idx * rows_dev
    same_group = group_ids[:, :, None] == group_ids[:, None, :]
    order_in = jnp.sum((same_group & earlier[None]).astype(jnp.int32), axis=2)
    count = jnp.sum((group_ids == serve_idx).astype(jnp.int32), axis=1)

    up = [(i, i + 1) for i in range(train_n - 1)]
    down = [(i + 1, i) for i in range(train_n - 1)]
    turned_weights = jnp.swapaxes(train_weights, 1, 2)

    def pack(c, after):
        base, per = firsts[c], sizes[c]
        low, high = base * PAIR, (base + per) * PAIR
        left = lax.ppermute(train_weights[low:high, buffer_len - SHIFT :], "train", up)
        right = lax.ppermute(train_weights[low:high, :SHIFT], "train", down)
        sent = pl.pallas_call(
            functools.partial(pack_kernel, base, slots_n),
            grid_spec=pltpu.PrefetchScalarGridSpec(
                num_scalar_prefetch=4,
                grid=(per,),
                in_specs=[
                    pl.BlockSpec((PAIR, columns, buffer_len), lambda p, *_: (base + p, 0, 0)),
                    pl.BlockSpec((PAIR, SHIFT, columns), lambda p, *_: (p, 0, 0)),
                    pl.BlockSpec((PAIR, SHIFT, columns), lambda p, *_: (p, 0, 0)),
                ]
                + [pl.BlockSpec(memory_space=pl.ANY)] * len(after),
                out_specs=pl.BlockSpec((serve_n, 1, pieces, BLOCK, LANES), lambda p, *_: (0, p, 0, 0, 0)),
                scratch_shapes=[
                    pltpu.VMEM((serve_n, PAIR * slots_n, BLOCK, LANES), dtype),
                    pltpu.VMEM((PAIR, buffer_len, columns), dtype),
                ],
            ),
            out_shape=jax.ShapeDtypeStruct((serve_n, per, pieces, BLOCK, LANES), dtype),
            cost_estimate=pl.CostEstimate(flops=0, bytes_accessed=12_000_000 * per, transcendentals=0),
            name=f"pack{c}",
        )(group_ids, order_in, first_row, next_row, turned_weights, left, right, *after)
        return lax.all_to_all(sent, "serve", split_axis=0, concat_axis=0, tiled=True)

    def unpack(c, received, held):
        base, per = firsts[c], sizes[c]
        return pl.pallas_call(
            functools.partial(unpack_kernel, base, slots_n, columns),
            grid_spec=pltpu.PrefetchScalarGridSpec(
                num_scalar_prefetch=1,
                grid=(per,),
                in_specs=[pl.BlockSpec((serve_n, 1, pieces, BLOCK, LANES), lambda p, *_: (0, p, 0, 0, 0))]
                + [pl.BlockSpec(memory_space=pl.ANY)] * len(held),
                out_specs=[
                    pl.BlockSpec((PAIR, slots_n, BLOCK, width), lambda p, *_: (base + p, 0, 0, 0)),
                    pl.BlockSpec((PAIR, slots_n, width), lambda p, *_: (base + p, 0, 0)),
                ],
                scratch_shapes=[
                    pltpu.VMEM((serve_n, BLOCK, LANES), jnp.float32),
                    pltpu.VMEM((serve_n, 1, LANES), jnp.float32),
                ],
            ),
            out_shape=[
                jax.ShapeDtypeStruct((layers, slots_n, BLOCK, width), dtype),
                jax.ShapeDtypeStruct((layers, slots_n, width), jnp.float32),
            ],
            input_output_aliases={2: 0, 3: 1} if held else {},
            cost_estimate=pl.CostEstimate(flops=0, bytes_accessed=12_000_000 * per, transcendentals=0),
            compiler_params=pltpu.CompilerParams(vmem_limit_bytes=24 * 1024 * 1024),
            name=f"unpack{c}",
        )(count, received, *held)

    outs, received = (), []
    for c in range(len(sizes)):
        if c >= 2:
            outs = unpack(c - 2, received[c - 2], outs)
        received.append(pack(c, outs[1:]))
    for c in range(max(0, len(sizes) - 2), len(sizes)):
        outs = unpack(c, received[c], outs)
    codes, scales = outs
    return (
        codes.reshape(layers, 1, 1, slots_n, BLOCK, width),
        scales.reshape(layers, 1, 1, slots_n, width),
    )


def solution(mesh):
    return jax.shard_map(
        shards,
        mesh=mesh,
        in_specs=(P(None, "train", "serve"), P(), P(None, "train", None)),
        out_specs=(
            P(None, "serve", "train", None, None, None),
            P(None, "serve", "train", None, None),
        ),
        check_vma=False,
    )
```

profile of v0, /device:TPU:1, one launch (start us, length us, event | category | flops | bytes accessed | tf_op | source)
XLA Modules:
  0.0 235.4 jit_solution(9624523535399740721)
XLA Ops:
  0.6 1.2 fusion.1
  2.0 4.0 %collective-permute-start.2 = (bf16[4,32,264]{2,1,0:T(8,128)(2,1)S(1)}, bf16[4,32,264]{2,1,0:T(8,128)(2,1)S(1)}, u32[]{:S(2)}, u32[]{:S(2)}) collective-permute-start(bf16[4,32,264]{2,1,0:T(8,128)(2,1)S(1)} %copy.27), channel_id=1, source_target_pairs={{0,8},{8,16},{16,24},{1,9},{9,17},{17,25},{2,10},{10,18},{18,26},{... | collective-permute-start | bytes 202760 | tf_op jit(solution)/shard_map/ppermute | solution.py:191
  6.2 1.3 collective-permute-start.3
  7.5 0.8 select_reduce_fusion
  8.3 0.6 broadcast_subtract_fusion
  8.9 1.9 convert_reduce_fusion.order_ref
  10.8 0.8 collective-permute-done.3.right_ref
  11.6 0.6 copy-done.4
  12.2 9.4 %pack0.1 = bf16[8,2,33,32,128]{4,3,2,1,0:T(8,128)(2,1)} custom-call(s32[16,56]{1,0:T(8,128)} %bitcast.14, s32[16,56]{1,0:T(8,128)} %convert_reduce_fusion.order_ref, s32[16]{0:T(128)} %get-tuple-element.27.first_ref, s32[16]{0:T(128)} %get-tuple-element.26.next_ref, bf16[16,264,1856]{2,1,0:T(8,128)(2,1)} %bitcast.8, bf16[4,32,264]{2,1,0:T(8,128)(2,1)} %copy-done.3, ...), custom_call_target="tpu_custom_call" | custom-call | bytes 24000000 | tf_op jit(solution)/shard_map/pack0/pallas_call | solution.py:193
  21.6 6.6 %all-to-all-start = ((bf16[8,2,33,32,128]{4,3,2,1,0:T(8,128)(2,1)}), bf16[8,2,33,32,128]{4,3,2,1,0:T(8,128)(2,1)}, u32[]{:S(2)}, u32[]{:S(2)}) async-start(bf16[8,2,33,32,128]{4,3,2,1,0:T(8,128)(2,1)} %pack0.1), calls=%async_computation | async-start | bytes 8650752 | tf_op jit(solution)/shard_map/all_to_all | solution.py:214
  28.1 1.6 fusion
  29.7 0.4 copy.29
  30.1 3.2 %collective-permute-start.4 = (bf16[10,32,264]{2,1,0:T(8,128)(2,1)S(1)}, bf16[10,32,264]{2,1,0:T(8,128)(2,1)S(1)}, u32[]{:S(2)}, u32[]{:S(2)}) collective-permute-start(bf16[10,32,264]{2,1,0:T(8,128)(2,1)S(1)} %copy.29), channel_id=1, source_target_pairs={{0,8},{8,16},{16,24},{1,9},{9,17},{17,25},{2,10},{10,18},{18,26},{... | collective-permute-start | bytes 506888 | tf_op jit(solution)/shard_map/ppermute | solution.py:191
  33.3 0.3 copy.30
  33.7 1.3 collective-permute-start.5
  35.0 3.5 %collective-permute-done.4.left_ref = bf16[10,32,264]{2,1,0:T(8,128)(2,1)S(1)} collective-permute-done((bf16[10,32,264]{2,1,0:T(8,128)(2,1)S(1)}, bf16[10,32,264]{2,1,0:T(8,128)(2,1)S(1)}, u32[]{:S(2)}, u32[]{:S(2)}) %collective-permute-start.4) | collective-permute-done | bytes 168992 | tf_op jit(solution)/shard_map/ppermute | solution.py:191
  38.5 4.2 %collective-permute-done.5.right_ref = bf16[10,32,264]{2,1,0:T(8,128)(2,1)S(1)} collective-permute-done((bf16[10,32,264]{2,1,0:T(8,128)(2,1)S(1)}, bf16[10,32,264]{2,1,0:T(8,128)(2,1)S(1)}, u32[]{:S(2)}, u32[]{:S(2)}) %collective-permute-start.5) | collective-permute-done | bytes 168992 | tf_op jit(solution)/shard_map/ppermute | solution.py:192
  42.7 0.7 copy-done.2
  43.4 17.8 %pack1.1 = bf16[8,5,33,32,128]{4,3,2,1,0:T(8,128)(2,1)} custom-call(s32[16,56]{1,0:T(8,128)} %bitcast.15, s32[16,56]{1,0:T(8,128)} %convert_reduce_fusion.order_ref, s32[16]{0:T(128)} %get-tuple-element.27.first_ref, s32[16]{0:T(128)} %get-tuple-element.26.next_ref, bf16[16,264,1856]{2,1,0:T(8,128)(2,1)} %bitcast.9, bf16[10,32,264]{2,1,0:T(8,128)(2,1)} %copy-done.1, ...), custom_call_target="tpu_custom_call" | custom-call | bytes 60000000 | tf_op jit(solution)/shard_map/pack1/pallas_call | solution.py:193
  61.2 14.0 %all-to-all-done.refs_0_ = bf16[8,2,33,32,128]{4,3,2,1,0:T(8,128)(2,1)} async-done(((bf16[8,2,33,32,128]{4,3,2,1,0:T(8,128)(2,1)}), bf16[8,2,33,32,128]{4,3,2,1,0:T(8,128)(2,1)}, u32[]{:S(2)}, u32[]{:S(2)}) %all-to-all-start) | async-done | bytes 4325408 | tf_op jit(solution)/shard_map/all_to_all | solution.py:214
  75.2 8.6 %all-to-all-start.2 = ((bf16[8,5,33,32,128]{4,3,2,1,0:T(8,128)(2,1)}), bf16[8,5,33,32,128]{4,3,2,1,0:T(8,128)(2,1)}, u32[]{:S(2)}, u32[]{:S(2)}) async-start(bf16[8,5,33,32,128]{4,3,2,1,0:T(8,128)(2,1)} %pack1.1), calls=%async_computation.2 | async-start | bytes 21626880 | tf_op jit(solution)/shard_map/all_to_all | solution.py:214
  83.8 1.1 fusion.2
  85.0 3.2 %collective-permute-start = (bf16[2,32,264]{2,1,0:T(8,128)(2,1)S(1)}, bf16[2,32,264]{2,1,0:T(8,128)(2,1)S(1)}, u32[]{:S(2)}, u32[]{:S(2)}) collective-permute-start(bf16[2,32,264]{2,1,0:T(8,128)(2,1)S(1)} %copy.25), channel_id=1, source_target_pairs={{0,8},{8,16},{16,24},{1,9},{9,17},{17,25},{2,10},{10,18},{18,26},{... | collective-permute-start | bytes 101384 | tf_op jit(solution)/shard_map/ppermute | solution.py:191
  88.4 1.3 collective-permute-start.1
  89.8 7.8 %unpack0.1 = (bf16[16,8,32,2112]{3,2,1,0:T(8,128)(2,1)}, f32[16,8,2112]{2,1,0:T(8,128)}) custom-call(s32[16]{0:T(128)S(1)} %convert_reduce_fusion.1.count_ref, bf16[8,2,33,32,128]{4,3,2,1,0:T(8,128)(2,1)} %all-to-all-done.refs_0_), custom_call_target="tpu_custom_call" | custom-call | bytes 24000000 | tf_op jit(solution)/shard_map/unpack0/pallas_call | solution.py:218
  97.7 0.6 copy-done.5
  98.3 6.6 %pack2.1 = bf16[8,1,33,32,128]{4,3,2,1,0:T(8,128)(2,1)} custom-call(s32[16,56]{1,0:T(8,128)} %bitcast.16, s32[16,56]{1,0:T(8,128)} %convert_reduce_fusion.order_ref, s32[16]{0:T(128)} %get-tuple-element.27.first_ref, s32[16]{0:T(128)} %get-tuple-element.26.next_ref, bf16[16,264,1856]{2,1,0:T(8,128)(2,1)} %bitcast.10, bf16[2,32,264]{2,1,0:T(8,128)(2,1)} %copy-done.5, ...), custom_call_target="tpu_custom_call" | custom-call | bytes 12000000 | tf_op jit(solution)/shard_map/pack2/pallas_call | solution.py:193
  104.9 95.5 %all-to-all-done.2.refs_0_ = bf16[8,5,33,32,128]{4,3,2,1,0:T(8,128)(2,1)} async-done(((bf16[8,5,33,32,128]{4,3,2,1,0:T(8,128)(2,1)}), bf16[8,5,33,32,128]{4,3,2,1,0:T(8,128)(2,1)}, u32[]{:S(2)}, u32[]{:S(2)}) %all-to-all-start.2) | async-done | bytes 10813472 | tf_op jit(solution)/shard_map/all_to_all | solution.py:214
  200.4 7.1 %all-to-all-start.1 = ((bf16[8,1,33,32,128]{4,3,2,1,0:T(8,128)(2,1)}), bf16[8,1,33,32,128]{4,3,2,1,0:T(8,128)(2,1)S(1)}, u32[]{:S(2)}, u32[]{:S(2)}) async-start(bf16[8,1,33,32,128]{4,3,2,1,0:T(8,128)(2,1)} %pack2.1), calls=%async_computation.1 | async-start | bytes 4325376 | tf_op jit(solution)/shard_map/all_to_all | solution.py:214
  207.5 14.9 %unpack1.1 = (bf16[16,8,32,2112]{3,2,1,0:T(8,128)(2,1)}, f32[16,8,2112]{2,1,0:T(8,128)}) custom-call(s32[16]{0:T(128)S(1)} %convert_reduce_fusion.1.count_ref, bf16[8,5,33,32,128]{4,3,2,1,0:T(8,128)(2,1)} %all-to-all-done.2.refs_0_, bf16[16,8,32,2112]{3,2,1,0:T(8,128)(2,1)} %get-tuple-element.9.refs_1_, ...), custom_call_target="tpu_custom_call", output_to_operand_aliasing={{0}: (2, {}), {1}: (3, {})} | custom-call | bytes 60000000 | tf_op jit(solution)/shard_map/unpack1/pallas_call | solution.py:218
  222.4 8.9 %all-to-all-done.1.refs_0_ = bf16[8,1,33,32,128]{4,3,2,1,0:T(8,128)(2,1)S(1)} async-done(((bf16[8,1,33,32,128]{4,3,2,1,0:T(8,128)(2,1)}), bf16[8,1,33,32,128]{4,3,2,1,0:T(8,128)(2,1)S(1)}, u32[]{:S(2)}, u32[]{:S(2)}) %all-to-all-start.1) | async-done | bytes 2162720 | tf_op jit(solution)/shard_map/all_to_all | solution.py:214
  231.3 4.1 %unpack2.1 = (bf16[16,8,32,2112]{3,2,1,0:T(8,128)(2,1)}, f32[16,8,2112]{2,1,0:T(8,128)}) custom-call(s32[16]{0:T(128)S(1)} %convert_reduce_fusion.1.count_ref, bf16[8,1,33,32,128]{4,3,2,1,0:T(8,128)(2,1)S(1)} %all-to-all-done.1.refs_0_, bf16[16,8,32,2112]{3,2,1,0:T(8,128)(2,1)} %get-tuple-element.10.refs_1_, ...), custom_call_target="tpu_custom_call", output_to_operand_aliasing={{0}: (2, {}), {1}: (3, {})} | custom-call | bytes 12000000 | tf_op jit(solution)/shard_map/unpack2/pallas_call | solution.py:218
  (22 shorter events, 0.8 us)
Async XLA Ops:
  2.0 8.8 %collective-permute-start.2 = (bf16[4,32,264]{2,1,0:T(8,128)(2,1)S(1)}, bf16[4,32,264]{2,1,0:T(8,128)(2,1)S(1)}, u32[]{:S(2)}, u32[]{:S(2)}) collective-permute-start(bf16[4,32,264]{2,1,0:T(8,128)(2,1)S(1)} %copy.27), channel_id=1, source_target_pairs={{0,8},{8,16},{16,24},{1,9},{9,17},{17,25},{2,10},{10,18},{18,26},{... | collective-permute-start | bytes 202760 | tf_op jit(solution)/shard_map/ppermute | solution.py:191
  6.2 5.4 %collective-permute-start.3 = (bf16[4,32,264]{2,1,0:T(8,128)(2,1)S(1)}, bf16[4,32,264]{2,1,0:T(8,128)(2,1)S(1)}, u32[]{:S(2)}, u32[]{:S(2)}) collective-permute-start(bf16[4,32,264]{2,1,0:T(8,128)(2,1)S(1)} %copy.28), channel_id=1, source_target_pairs={{8,0},{16,8},{24,16},{9,1},{17,9},{25,17},{10,2},{18,10},{26,18},{... | collective-permute-start | bytes 202760 | tf_op jit(solution)/shard_map/ppermute | solution.py:192
  10.8 0.8 copy-start.3
  11.5 0.6 copy-start.4
  21.6 53.6 %all-to-all-start = ((bf16[8,2,33,32,128]{4,3,2,1,0:T(8,128)(2,1)}), bf16[8,2,33,32,128]{4,3,2,1,0:T(8,128)(2,1)}, u32[]{:S(2)}, u32[]{:S(2)}) async-start(bf16[8,2,33,32,128]{4,3,2,1,0:T(8,128)(2,1)} %pack0.1), calls=%async_computation | async-start | bytes 8650752 | tf_op jit(solution)/shard_map/all_to_all | solution.py:214
  30.1 8.4 %collective-permute-start.4 = (bf16[10,32,264]{2,1,0:T(8,128)(2,1)S(1)}, bf16[10,32,264]{2,1,0:T(8,128)(2,1)S(1)}, u32[]{:S(2)}, u32[]{:S(2)}) collective-permute-start(bf16[10,32,264]{2,1,0:T(8,128)(2,1)S(1)} %copy.29), channel_id=1, source_target_pairs={{0,8},{8,16},{16,24},{1,9},{9,17},{17,25},{2,10},{10,18},{18,26},{... | collective-permute-start | bytes 506888 | tf_op jit(solution)/shard_map/ppermute | solution.py:191
  33.7 9.0 %collective-permute-start.5 = (bf16[10,32,264]{2,1,0:T(8,128)(2,1)S(1)}, bf16[10,32,264]{2,1,0:T(8,128)(2,1)S(1)}, u32[]{:S(2)}, u32[]{:S(2)}) collective-permute-start(bf16[10,32,264]{2,1,0:T(8,128)(2,1)S(1)} %copy.30), channel_id=1, source_target_pairs={{8,0},{16,8},{24,16},{9,1},{17,9},{25,17},{10,2},{18,10},{26,18},{... | collective-permute-start | bytes 506888 | tf_op jit(solution)/shard_map/ppermute | solution.py:192
  38.5 4.2 %copy-start.1 = (bf16[10,32,264]{2,1,0:T(8,128)(2,1)}, bf16[10,32,264]{2,1,0:T(8,128)(2,1)S(1)}, u32[]{:S(2)}) copy-start(bf16[10,32,264]{2,1,0:T(8,128)(2,1)S(1)} %collective-permute-done.4.left_ref) | copy-start | bytes 506884
  42.7 0.7 copy-start.2
  61.2 28.5 %copy-start = (s32[16,56,1]{1,2,0:T(1,128)S(1)}, s32[16,56,1]{1,2,0:T(1,128)}, u32[]{:S(2)}) copy-start(s32[16,56,1]{1,2,0:T(1,128)} %param.5) | copy-start | bytes 10756
  75.2 125.2 %all-to-all-start.2 = ((bf16[8,5,33,32,128]{4,3,2,1,0:T(8,128)(2,1)}), bf16[8,5,33,32,128]{4,3,2,1,0:T(8,128)(2,1)}, u32[]{:S(2)}, u32[]{:S(2)}) async-start(bf16[8,5,33,32,128]{4,3,2,1,0:T(8,128)(2,1)} %pack1.1), calls=%async_computation.2 | async-start | bytes 21626880 | tf_op jit(solution)/shard_map/all_to_all | solution.py:214
  85.0 12.6 %collective-permute-start = (bf16[2,32,264]{2,1,0:T(8,128)(2,1)S(1)}, bf16[2,32,264]{2,1,0:T(8,128)(2,1)S(1)}, u32[]{:S(2)}, u32[]{:S(2)}) collective-permute-start(bf16[2,32,264]{2,1,0:T(8,128)(2,1)S(1)} %copy.25), channel_id=1, source_target_pairs={{0,8},{8,16},{16,24},{1,9},{9,17},{17,25},{2,10},{10,18},{18,26},{... | collective-permute-start | bytes 101384 | tf_op jit(solution)/shard_map/ppermute | solution.py:191
  88.4 9.3 %collective-permute-start.1 = (bf16[2,32,264]{2,1,0:T(8,128)(2,1)S(1)}, bf16[2,32,264]{2,1,0:T(8,128)(2,1)S(1)}, u32[]{:S(2)}, u32[]{:S(2)}) collective-permute-start(bf16[2,32,264]{2,1,0:T(8,128)(2,1)S(1)} %copy.26), channel_id=1, source_target_pairs={{8,0},{16,8},{24,16},{9,1},{17,9},{25,17},{10,2},{18,10},{26,18},{... | collective-permute-start | bytes 101384 | tf_op jit(solution)/shard_map/ppermute | solution.py:192
  97.6 0.6 copy-start.5
  97.6 0.6 copy-start.6
  200.4 31.0 %all-to-all-start.1 = ((bf16[8,1,33,32,128]{4,3,2,1,0:T(8,128)(2,1)}), bf16[8,1,33,32,128]{4,3,2,1,0:T(8,128)(2,1)S(1)}, u32[]{:S(2)}, u32[]{:S(2)}) async-start(bf16[8,1,33,32,128]{4,3,2,1,0:T(8,128)(2,1)} %pack2.1), calls=%async_computation.1 | async-start | bytes 4325376 | tf_op jit(solution)/shard_map/all_to_all | solution.py:214
where the time goes:
time: 240 us; the launch traced here: 235 us
  waiting for transfers between devices  127 us (53%)
  Pallas kernels  60.7 us (25%)
  starting transfers between devices  36.6 us (15%)
  local copies, waits for them, and re-layouts  7.1 us (3%)
  other arithmetic  3.38 us (1%)
    all_to_all x3, waiting for transfers between devices, pack(): lax.all_to_all(sent, 'serve', split_axis=0, concat_axis=0, tiled=True)  118 us
    pallas_call x3, Pallas kernels, pack(): pl.pallas_call(functools.partial(pack_kernel, base, slots_n), grid_spec=p...  33.8 us
    pallas_call x3, Pallas kernels, unpack(): pl.pallas_call(functools.partial(unpack_kernel, base, slots_n, columns),...  26.8 us
    all_to_all x3, starting transfers between devices, pack(): lax.all_to_all(sent, 'serve', split_axis=0, concat_axis=0, tiled=True)  22.3 us
    ppermute x3, starting transfers between devices, pack(): lax.ppermute(train_weights[low:high, buffer_len - SHIFT:], 'train', up)  10.4 us
    ppermute x3, waiting for transfers between devices, pack(): right = lax.ppermute(train_weights[low:high, :SHIFT], 'train', down)  4.96 us
  transfers between devices with their start and end apart: 9, of which 6 were waited for; matrix products, arithmetic and copies ran while one was open for 3% of the time, Pallas kernels for 20%

commit v1 on v0

v1 whole, which is shorter than its diff:
```python
import functools

import jax
import jax.numpy as jnp
from jax import lax
from jax.experimental import pallas as pl
from jax.experimental.pallas import tpu as pltpu
from jax.sharding import PartitionSpec as P

BLOCK = 32
SHIFT = 32
LANES = 128
PAIR = 2
MESH = pl.DeviceIdType.MESH
MIB = 1024 * 1024


def turned(values):
    return jnp.transpose(values.astype(jnp.float32))


def partner(me, mask, count):
    out, bit = 0, 1
    while bit < count:
        out = out + ((me // bit + mask // bit) % 2) * bit
        bit *= 2
    return out


def scaled(values):
    values = values.astype(jnp.float32)
    divisor = jnp.maximum(jnp.max(jnp.abs(values), axis=0, keepdims=True), 0.25)
    return values * (1.0 / divisor), divisor


def unpack_pair(dims, recv, rem_code, rem_scale, rows, put_code, put_scale):
    slots, full, rem, columns, sources = dims
    width = columns * sources
    tiles = -(-width // LANES)
    lane = lax.broadcasted_iota(jnp.int32, (BLOCK, LANES), 1)
    lane_row = lax.broadcasted_iota(jnp.int32, (1, LANES), 1)
    if rem:
        for s in range(sources):
            rem_code[s], rem_scale[s] = scaled(recv(s, PAIR * slots * full))

    def slot(i, carry):
        parts = [None] * tiles

        def put(tile, low, code, scale):
            if tile >= tiles:
                return
            if parts[tile] is None:
                parts[tile] = (code, scale)
            else:
                before = parts[tile]
                parts[tile] = (jnp.where(lane >= low, code, before[0]), jnp.where(lane_row >= low, scale, before[1]))

        def flush(below):
            for tile in range(below):
                if parts[tile] is not None:
                    code, scale = parts[tile]
                    end = min(width, (tile + 1) * LANES)
                    size = end - tile * LANES
                    put_code(i, tile * LANES, end, code[:, :size])
                    rows[i, :, tile * LANES : end] = scale[:, :size]
                    parts[tile] = None

        for s in range(sources):
            for t in range(full + (1 if rem else 0)):
                start = s * columns + t * LANES
                size = LANES if t < full else rem
                low = start % LANES
                if t < full:
                    code, scale = scaled(recv(s, i * full + t))
                    if low:
                        code, scale = pltpu.roll(code, low, 1), pltpu.roll(scale, low, 1)
                else:
                    turn = lax.rem(low + LANES - i * rem, LANES)
                    code, scale = pltpu.roll(rem_code[s], turn, 1), pltpu.roll(rem_scale[s], turn, 1)
                tile = start // LANES
                put(tile, low, code, scale)
                if low + size > LANES:
                    put(tile + 1, 0, code, scale)
                flush((start + size) // LANES)
        flush(tiles)
        return carry

    lax.fori_loop(0, PAIR * slots, slot, 0)
    for i in range(PAIR * slots):
        put_scale(i // slots, i % slots, rows[i])


def move_kernel(
    dims,
    table_ref,
    offset_ref,
    wt_ref,
    codes_ref,
    scale_ref,
    recv_ref,
    send_ref,
    in_ref,
    w_ref,
    rem_ref,
    edge_ref,
    halo_ref,
    rem_code,
    rem_scale,
    rows,
    in_sem,
    send_sem,
    recv_sem,
    halo_send,
    halo_recv,
):
    slots, full, rem, columns, groups = dims
    pairs = recv_ref.shape[1]
    layers = pairs * PAIR
    blocks = w_ref.shape[0]
    buffer_len = blocks * BLOCK
    rows_dev = buffer_len - 2 * SHIFT
    me = lax.axis_index("serve")
    part = lax.axis_index("train")
    parts_n = lax.axis_size("train")
    half = slots * full
    rest = half + (1 if rem else 0)

    def fetch(layer, sub):
        return pltpu.make_async_copy(wt_ref.at[layer], in_ref.at[sub], in_sem.at[sub])

    def message(mask, pair, sub):
        peer = partner(me, mask, groups)
        span = pl.ds(sub * half, rest if sub == PAIR - 1 else half)
        return pltpu.make_async_remote_copy(
            send_ref.at[peer, pair, span],
            recv_ref.at[me, pair, span],
            send_sem.at[mask, pair, sub],
            recv_sem.at[mask, pair, sub],
            device_id={"serve": peer},
            device_id_type=MESH,
        )

    def arrival(mask, pair, sub):
        peer = partner(me, mask, groups)
        span = pl.ds(sub * half, rest if sub == PAIR - 1 else half)
        return pltpu.make_async_remote_copy(
            recv_ref.at[peer, pair, span],
            recv_ref.at[peer, pair, span],
            send_sem.at[mask, pair, sub],
            recv_sem.at[mask, pair, sub],
            device_id={"serve": peer},
            device_id_type=MESH,
        )

    def edge(layer, side):
        to = part + 1 if side == 0 else part - 1
        return pltpu.make_async_remote_copy(
            edge_ref.at[layer, side],
            halo_ref.at[layer, side],
            halo_send.at[layer, side],
            halo_recv.at[layer, side],
            device_id={"train": to},
            device_id_type=MESH,
        )

    for sub in range(PAIR):
        fetch(sub, sub).start()

    barrier = pltpu.get_barrier_semaphore()

    def greet(mask, carry):
        pl.semaphore_signal(barrier, inc=1, device_id={"serve": partner(me, mask, groups)}, device_id_type=MESH)
        return carry

    lax.fori_loop(1, groups, greet, 0)

    @pl.when(part > 0)
    def _():
        pl.semaphore_signal(barrier, inc=1, device_id={"train": part - 1}, device_id_type=MESH)

    @pl.when(part < parts_n - 1)
    def _():
        pl.semaphore_signal(barrier, inc=1, device_id={"train": part + 1}, device_id_type=MESH)

    below = (part + parts_n - 1) // parts_n
    above = (2 * parts_n - 2 - part) // parts_n
    pl.semaphore_wait(barrier, groups - 1 + below + above)

    row = lax.broadcasted_iota(jnp.int32, (BLOCK, columns), 0)
    lane = lax.broadcasted_iota(jnp.int32, (BLOCK, LANES), 1)
    last = rows_dev - BLOCK

    def transpose_tile(sub, low):
        high = min(low + LANES, buffer_len)
        rows_of = turned(in_ref[sub, :, low:high]).astype(w_ref.dtype)
        w_ref[low // BLOCK : high // BLOCK] = rows_of.reshape((high - low) // BLOCK, BLOCK, columns)

    def pack_layer(pair, sub):
        layer = pair * PAIR + sub
        fetch(layer, sub).wait()
        lows = list(range(0, buffer_len, LANES))
        lows = [lows[0], lows[-1]] + lows[1:-1]
        for low in lows[:2]:
            transpose_tile(sub, low)
        edge_ref[layer, 0] = w_ref[blocks - 1]
        edge_ref[layer, 1] = w_ref[0]

        @pl.when(part < parts_n - 1)
        def _():
            edge(layer, 0).start()

        @pl.when(part > 0)
        def _():
            edge(layer, 1).start()

        for low in lows[2:]:
            transpose_tile(sub, low)

        @pl.when(layer + PAIR < layers)
        def _():
            fetch(layer + PAIR, sub).start()

        base = part * rows_dev

        @pl.when(part > 0)
        def _():
            edge(layer, 0).wait_recv()
            first = offset_ref[part, layer] - base
            head = jnp.where(row < first, halo_ref[layer, 0].astype(jnp.float32), w_ref[1].astype(jnp.float32))
            w_ref[1] = head.astype(w_ref.dtype)

        @pl.when(part < parts_n - 1)
        def _():
            edge(layer, 1).wait_recv()
            after = offset_ref[part + 1, layer] - base
            tail = w_ref[blocks - 2].astype(jnp.float32)
            tail = jnp.where(row + last >= after, halo_ref[layer, 1].astype(jnp.float32), tail)
            w_ref[blocks - 2] = tail.astype(w_ref.dtype)

        w_ref[0] = jnp.zeros((BLOCK, columns), w_ref.dtype)

        def gather(group, out):
            for k in range(slots):
                block = w_ref[table_ref[layer, group * slots + k]]
                for t in range(full):
                    out[pair, (sub * slots + k) * full + t] = block[:, t * LANES : (t + 1) * LANES]
                if rem:
                    rem_ref[group, sub * slots + k, :, 0:rem] = block[:, full * LANES :]
            if rem and sub == PAIR - 1:
                tile = rem_ref[group, 0].astype(jnp.float32)
                for i in range(1, PAIR * slots):
                    moved = pltpu.roll(rem_ref[group, i].astype(jnp.float32), i * rem, 1)
                    tile = jnp.where(lane >= i * rem, moved, tile)
                out[pair, PAIR * half] = tile.astype(out.dtype)

        def give(mask, carry):
            peer = partner(me, mask, groups)
            gather(peer, send_ref.at[peer])
            message(mask, pair, sub).start()
            return carry

        lax.fori_loop(2, groups, give, 0)
        give(1, 0)
        gather(me, recv_ref.at[me])

    def take(pair):
        for sub in range(PAIR):

            def arrive(mask, carry, sub=sub):
                arrival(mask, pair, sub).wait_recv()
                return carry

            lax.fori_loop(1, groups, arrive, 0)

    def unpack(pair):
        def put_code(i, low, high, code):
            codes_ref[pair * PAIR + i // slots, i % slots, :, low:high] = code.astype(codes_ref.dtype)

        def put_scale(sub, k, scale):
            scale_ref[pair * PAIR + sub, k : k + 1, :] = scale

        unpack_pair(dims, lambda s, n: recv_ref[s, pair, n], rem_code, rem_scale, rows, put_code, put_scale)

    def step(pair, carry):
        for sub in range(PAIR):
            pack_layer(pair, sub)

        @pl.when(pair > 0)
        def _():
            take(pair - 1)
            unpack(pair - 1)

        return carry

    lax.fori_loop(0, pairs, step, 0)
    take(pairs - 1)

    def drain(pair, carry):
        for sub in range(PAIR):

            def sent(mask, inner, sub=sub):
                message(mask, pair, sub).wait_send()
                return inner

            lax.fori_loop(1, groups, sent, 0)
            layer = pair * PAIR + sub

            @pl.when(part < parts_n - 1)
            def _(layer=layer):
                edge(layer, 0).wait_send()

            @pl.when(part > 0)
            def _(layer=layer):
                edge(layer, 1).wait_send()

        return carry

    lax.fori_loop(0, pairs, drain, 0)


def write_kernel(
    dims, table_ref, codes_ref, scale_ref, recv_ref, codes_out, scale_out, codes, scales, rem_code, rem_scale, rows, sems
):
    slots = dims[0]
    layers = codes_ref.shape[0]
    done = layers - PAIR
    pair = recv_ref.shape[1] - 1
    me = lax.axis_index("serve")
    copies = [pltpu.make_async_copy(codes_ref.at[n], codes_out.at[n], sems.at[n]) for n in range(done)]
    for copy in copies:
        copy.start()

    def put_code(i, low, high, code):
        codes[i // slots, i % slots, :, low:high] = code.astype(codes.dtype)

    def mask(layer, k, scale):
        return jnp.where(table_ref[layer, me * slots + k] > 0, scale, 0.0)

    def put_scale(sub, k, scale):
        scales[done + sub, k : k + 1, :] = mask(done + sub, k, scale)

    unpack_pair(dims, lambda s, n: recv_ref[s, pair, n], rem_code, rem_scale, rows, put_code, put_scale)
    tail = [
        pltpu.make_async_copy(codes, codes_out.at[pl.ds(done, PAIR)], sems.at[done]),
        pltpu.make_async_copy(scales, scale_out, sems.at[done + 1]),
    ]
    tail[0].start()

    def masked(layer, carry):
        for k in range(slots):
            scales[layer, k : k + 1, :] = mask(layer, k, scale_ref[layer, k : k + 1, :])
        return carry

    lax.fori_loop(0, done, masked, 0)
    tail[1].start()
    for copy in copies + tail:
        copy.wait()


def shards(train_weights, row_offset, block_group):
    train_n = lax.axis_size("train")
    serve_n = lax.axis_size("serve")
    layers, buffer_len, columns = train_weights.shape
    blocks_dev = block_group.shape[1]
    slots = (blocks_dev + serve_n - 1) // serve_n + 1
    full = columns // LANES
    rem = columns - full * LANES
    pairs = layers // PAIR
    pieces = PAIR * slots * full + (1 if rem else 0)
    width = columns * serve_n
    dtype = train_weights.dtype
    dims = (slots, full, rem, columns, serve_n)
    assert SHIFT == BLOCK and buffer_len % BLOCK == 0
    assert PAIR * slots * rem <= LANES and layers % PAIR == 0

    position = jnp.arange(blocks_dev, dtype=jnp.int32)
    earlier = position[None, :] < position[:, None]
    group_ids = block_group[:, :, 0]
    same_group = group_ids[:, :, None] == group_ids[:, None, :]
    order_in = jnp.sum((same_group & earlier[None]).astype(jnp.int32), axis=2)
    place = group_ids * slots + order_in
    slot_ids = jnp.arange(serve_n * slots, dtype=jnp.int32)
    hit = place[:, None, :] == slot_ids[None, :, None]
    table = jnp.sum(jnp.where(hit, position[None, None, :] + 1, 0), axis=2)

    smem = pl.BlockSpec(memory_space=pltpu.SMEM)
    vmem = pl.BlockSpec(memory_space=pltpu.VMEM)
    anywhere = pl.BlockSpec(memory_space=pl.ANY)
    codes, scales, received = pl.pallas_call(
        functools.partial(move_kernel, dims),
        in_specs=[smem, smem, anywhere],
        out_specs=[vmem, vmem, vmem],
        out_shape=[
            pltpu.VMEM((layers, slots, BLOCK, width), dtype),
            pltpu.VMEM((layers, slots, width), jnp.float32),
            pltpu.VMEM((serve_n, pairs, pieces, BLOCK, LANES), dtype),
        ],
        scratch_shapes=[
            pltpu.VMEM((serve_n, pairs, pieces, BLOCK, LANES), dtype),
            pltpu.VMEM((PAIR, columns, buffer_len), dtype),
            pltpu.VMEM((buffer_len // BLOCK, BLOCK, columns), dtype),
            pltpu.VMEM((serve_n, PAIR * slots, BLOCK, LANES), dtype),
            pltpu.VMEM((layers, 2, SHIFT, columns), dtype),
            pltpu.VMEM((layers, 2, SHIFT, columns), dtype),
            pltpu.VMEM((serve_n, BLOCK, LANES), jnp.float32),
            pltpu.VMEM((serve_n, 1, LANES), jnp.float32),
            pltpu.VMEM((PAIR * slots, 1, width), jnp.float32),
            pltpu.SemaphoreType.DMA((PAIR,)),
            pltpu.SemaphoreType.DMA((serve_n, pairs, PAIR)),
            pltpu.SemaphoreType.DMA((serve_n, pairs, PAIR)),
            pltpu.SemaphoreType.DMA((layers, 2)),
            pltpu.SemaphoreType.DMA((layers, 2)),
        ],
        compiler_params=pltpu.CompilerParams(
            collective_id=0, has_side_effects=True, vmem_limit_bytes=26 * MIB
        ),
        name="move",
    )(table, row_offset.T, jnp.swapaxes(train_weights, 1, 2))

    codes_out, scales_out = pl.pallas_call(
        functools.partial(write_kernel, dims),
        in_specs=[smem, vmem, vmem, vmem],
        out_specs=[pl.BlockSpec(memory_space=pltpu.HBM)] * 2,
        out_shape=[
            jax.ShapeDtypeStruct((layers, slots, BLOCK, width), dtype),
            jax.ShapeDtypeStruct((layers, slots, width), jnp.float32),
        ],
        scratch_shapes=[
            pltpu.VMEM((PAIR, slots, BLOCK, width), dtype),
            pltpu.VMEM((layers, slots, width), jnp.float32),
            pltpu.VMEM((serve_n, BLOCK, LANES), jnp.float32),
            pltpu.VMEM((serve_n, 1, LANES), jnp.float32),
            pltpu.VMEM((PAIR * slots, 1, width), jnp.float32),
            pltpu.SemaphoreType.DMA((layers,)),
        ],
        compiler_params=pltpu.CompilerParams(vmem_limit_bytes=6 * MIB),
        name="write",
    )(table, codes, scales, received)
    return (
        codes_out.reshape(layers, 1, 1, slots, BLOCK, width),
        scales_out.reshape(layers, 1, 1, slots, width),
    )


def solution(mesh):
    return jax.shard_map(
        shards,
        mesh=mesh,
        in_specs=(P(None, "train", "serve"), P(), P(None, "train", None)),
        out_specs=(
            P(None, "serve", "train", None, None, None),
            P(None, "serve", "train", None, None),
        ),
        check_vma=False,
    )
```

time: 240 us -> 223 us (0.929); the launches traced: 235 us -> 223 us
  Pallas kernels: 60.7 us -> 206 us
  waiting for transfers between devices: 127 us -> 0 us
  starting transfers between devices: 36.6 us -> 0 us
  local copies, waits for them, and re-layouts: 7.1 us -> 13.3 us
    pallas_call x6 -> x2, Pallas kernels: 60.7 us -> 206 us  [the longest x1 199 us: shards(): pl.pallas_call(functools.partial(move_kernel, dims), in_specs=[smem, smem...]
    all_to_all x3 -> x0, waiting for transfers between devices: 118 us -> none  [pack(): lax.all_to_all(sent, 'serve', split_axis=0, concat_axis=0, tiled=True)]
    all_to_all x3 -> x0, starting transfers between devices: 22.3 us -> none  [pack(): lax.all_to_all(sent, 'serve', split_axis=0, concat_axis=0, tiled=True)]
    ppermute x6 -> x0, starting transfers between devices: 14.3 us -> none  [the longest x3 10.4 us: pack(): lax.ppermute(train_weights[low:high, buffer_len - SHIFT:], 'train', up)]
    unnamed x20 -> x6, local copies, waits for them, and re-layouts: 3.26 us -> 13.3 us
    ppermute x6 -> x0, waiting for transfers between devices: 8.45 us -> none  [the longest x3 4.96 us: pack(): right = lax.ppermute(train_weights[low:high, :SHIFT], 'train', down)]
    slice x3 -> x0, local copies, waits for them, and re-layouts: 3.83 us -> none  [pack(): right = lax.ppermute(train_weights[low:high, :SHIFT], 'train', down)]
  transfers between devices with their start and end apart: 9 -> 0, of which waited for: 6 -> 0; matrix products, arithmetic and copies ran while one was open for 3% -> 0% of each run, Pallas kernels for 20% -> 0%
where the time goes in v1:
time: 223 us
  Pallas kernels  206 us (92%)
  local copies, waits for them, and re-layouts  13.3 us (6%)
  other arithmetic  2.81 us (1%)
    pallas_call x1, Pallas kernels, shards(): pl.pallas_call(functools.partial(move_kernel, dims), in_specs=[smem, smem...  199 us
    unnamed x6, local copies, waits for them, and re-layouts  13.3 us
    pallas_call x1, Pallas kernels, shards(): pl.pallas_call(functools.partial(write_kernel, dims), in_specs=[smem, vme...  7.28 us

profile of v1, /device:TPU:1, one launch (start us, length us, event | category | flops | bytes accessed | tf_op | source)
XLA Modules:
  0.0 222.9 jit_solution(7786428410812975144)
XLA Ops:
  0.7 1.3 convert_reduce_fusion
  1.9 0.7 multiply_add_fusion
  2.6 0.8 select_reduce_fusion.table_ref
  3.5 198.9 %move.1 = (bf16[16,8,32,2112]{3,2,1,0:T(8,128)(2,1)S(1)}, f32[16,8,2112]{2,1,0:T(8,128)S(1)}, bf16[8,8,33,32,128]{4,3,2,1,0:T(8,128)(2,1)S(1)}) custom-call(s32[16,64]{1,0:T(8,128)} %select_reduce_fusion.table_ref, s32[5,16]{1,0:T(8,128)} %bitcast.12, bf16[16,264,1856]{2,1,0:T(8,128)(2,1)} %bitcast.9), custom_call_target="tpu_custom_call" | custom-call | tf_op jit(solution)/shard_map/move/pallas_call | solution.py:389
  202.3 0.0 copy-start
  202.4 6.5 %copy-done = bf16[16,8,32,2112]{3,2,1,0:T(8,128)(2,1)} copy-done((bf16[16,8,32,2112]{3,2,1,0:T(8,128)(2,1)}, bf16[16,8,32,2112]{3,2,1,0:T(8,128)(2,1)S(1)}, u32[]{:S(2)}) %copy-start) | copy-done | bytes 17301528
  208.8 0.0 copy-start.1
  208.9 6.1 %copy-done.1 = bf16[16,8,32,2112]{3,2,1,0:T(8,128)(2,1)S(1)} copy-done((bf16[16,8,32,2112]{3,2,1,0:T(8,128)(2,1)S(1)}, bf16[16,8,32,2112]{3,2,1,0:T(8,128)(2,1)}, u32[]{:S(2)}) %copy-start.1) | copy-done | bytes 17301528
  214.9 0.0 copy-start.2
  214.9 0.7 copy-done.2
  215.6 7.3 %write.1 = (bf16[16,8,32,2112]{3,2,1,0:T(8,128)(2,1)}, f32[16,8,2112]{2,1,0:T(8,128)}) custom-call(s32[16,64]{1,0:T(8,128)S(1)} %copy-done.2, bf16[16,8,32,2112]{3,2,1,0:T(8,128)(2,1)S(1)} %copy-done.1, f32[16,8,2112]{2,1,0:T(8,128)S(1)} %get-tuple-element.8.scale_ref, bf16[8,8,33,32,128]{4,3,2,1,0:T(8,128)(2,1)S(1)} %get-tuple-element.9.recv_ref), custom_call_target="tpu_custom_call" | custom-call | tf_op jit(solution)/shard_map/write/pallas_call | solution.py:420
  (2 shorter events, 0.0 us)
Async XLA Ops:
  202.3 6.5 %copy-start = (bf16[16,8,32,2112]{3,2,1,0:T(8,128)(2,1)}, bf16[16,8,32,2112]{3,2,1,0:T(8,128)(2,1)S(1)}, u32[]{:S(2)}) copy-start(bf16[16,8,32,2112]{3,2,1,0:T(8,128)(2,1)S(1)} %get-tuple-element.7.codes_ref) | copy-start | bytes 51904516
  208.8 6.1 %copy-start.1 = (bf16[16,8,32,2112]{3,2,1,0:T(8,128)(2,1)S(1)}, bf16[16,8,32,2112]{3,2,1,0:T(8,128)(2,1)}, u32[]{:S(2)}) copy-start(bf16[16,8,32,2112]{3,2,1,0:T(8,128)(2,1)} %copy-done) | copy-start | bytes 51904516
  214.9 0.7 copy-start.2

commit v2 on v1

--- a/solution.py
+++ b/solution.py
@@ -11,6 +11,7 @@
 SHIFT = 32
 LANES = 128
 PAIR = 2
+RING = 3
 MESH = pl.DeviceIdType.MESH
 MIB = 1024 * 1024
 
@@ -92,8 +93,8 @@
 
 def move_kernel(
     dims,
-    table_ref,
     offset_ref,
+    group_ref,
     wt_ref,
     codes_ref,
     scale_ref,
@@ -107,7 +108,10 @@
     rem_code,
     rem_scale,
     rows,
+    table_ref,
+    table_smem,
     in_sem,
+    table_sem,
     send_sem,
     recv_sem,
     halo_send,
@@ -132,9 +136,9 @@
         peer = partner(me, mask, groups)
         span = pl.ds(sub * half, rest if sub == PAIR - 1 else half)
         return pltpu.make_async_remote_copy(
-            send_ref.at[peer, pair, span],
+            send_ref.at[peer, pair % RING, span],
             recv_ref.at[me, pair, span],
-            send_sem.at[mask, pair, sub],
+            send_sem.at[mask, pair % RING, sub],
             recv_sem.at[mask, pair, sub],
             device_id={"serve": peer},
             device_id_type=MESH,
@@ -146,7 +150,7 @@
         return pltpu.make_async_remote_copy(
             recv_ref.at[peer, pair, span],
             recv_ref.at[peer, pair, span],
-            send_sem.at[mask, pair, sub],
+            send_sem.at[mask, pair % RING, sub],
             recv_sem.at[mask, pair, sub],
             device_id={"serve": peer},
             device_id_type=MESH,
@@ -184,7 +188,23 @@
 
     below = (part + parts_n - 1) // parts_n
     above = (2 * parts_n - 2 - part) // parts_n
+
+    spot = lax.broadcasted_iota(jnp.int32, table_ref.shape, 1)
+    spot_group = jnp.zeros(table_ref.shape, jnp.int32)
+    for g in range(1, groups):
+        spot_group = spot_group + jnp.where(spot >= g * slots, 1, 0)
+    spot_slot = spot - spot_group * slots
+    seen = jnp.zeros(table_ref.shape, jnp.int32)
+    table = jnp.zeros(table_ref.shape, jnp.int32)
+    for j in range(group_ref.shape[1]):
+        mine = group_ref[:, j : j + 1] == spot_group
+        table = jnp.where(mine & (seen == spot_slot), j + 1, table)
+        seen = jnp.where(mine, seen + 1, seen)
+    table_ref[...] = table
+    to_smem = pltpu.make_async_copy(table_ref, table_smem, table_sem)
+    to_smem.start()
     pl.semaphore_wait(barrier, groups - 1 + below + above)
+    to_smem.wait()
 
     row = lax.broadcasted_iota(jnp.int32, (BLOCK, columns), 0)
     lane = lax.broadcasted_iota(jnp.int32, (BLOCK, LANES), 1)
@@ -241,9 +261,9 @@
 
         def gather(group, out):
             for k in range(slots):
-                block = w_ref[table_ref[layer, group * slots + k]]
+                block = w_ref[table_smem[layer, group * slots + k]]
                 for t in range(full):
-                    out[pair, (sub * slots + k) * full + t] = block[:, t * LANES : (t + 1) * LANES]
+                    out[(sub * slots + k) * full + t] = block[:, t * LANES : (t + 1) * LANES]
                 if rem:
                     rem_ref[group, sub * slots + k, :, 0:rem] = block[:, full * LANES :]
             if rem and sub == PAIR - 1:
@@ -251,17 +271,17 @@
                 for i in range(1, PAIR * slots):
                     moved = pltpu.roll(rem_ref[group, i].astype(jnp.float32), i * rem, 1)
                     tile = jnp.where(lane >= i * rem, moved, tile)
-                out[pair, PAIR * half] = tile.astype(out.dtype)
+                out[PAIR * half] = tile.astype(out.dtype)
 
         def give(mask, carry):
             peer = partner(me, mask, groups)
-            gather(peer, send_ref.at[peer])
+            gather(peer, send_ref.at[peer, pair % RING])
             message(mask, pair, sub).start()
             return carry
 
         lax.fori_loop(2, groups, give, 0)
         give(1, 0)
-        gather(me, recv_ref.at[me])
+        gather(me, recv_ref.at[me, pair])
 
     def take(pair):
         for sub in range(PAIR):
@@ -281,7 +301,20 @@
 
         unpack_pair(dims, lambda s, n: recv_ref[s, pair, n], rem_code, rem_scale, rows, put_code, put_scale)
 
+    def sent(pair):
+        for sub in range(PAIR):
+
+            def leave(mask, carry, sub=sub):
+                message(mask, pair, sub).wait_send()
+                return carry
+
+            lax.fori_loop(1, groups, leave, 0)
+
     def step(pair, carry):
+        @pl.when(pair >= RING)
+        def _():
+            sent(pair - RING)
+
         for sub in range(PAIR):
             pack_layer(pair, sub)
 
@@ -294,66 +327,41 @@
 
     lax.fori_loop(0, pairs, step, 0)
     take(pairs - 1)
+    unpack(pairs - 1)
 
     def drain(pair, carry):
-        for sub in range(PAIR):
-
-            def sent(mask, inner, sub=sub):
-                message(mask, pair, sub).wait_send()
-                return inner
-
-            lax.fori_loop(1, groups, sent, 0)
-            layer = pair * PAIR + sub
-
-            @pl.when(part < parts_n - 1)
-            def _(layer=layer):
-                edge(layer, 0).wait_send()
-
-            @pl.when(part > 0)
-            def _(layer=layer):
-                edge(layer, 1).wait_send()
-
+        sent(pair)
         return carry
 
-    lax.fori_loop(0, pairs, drain, 0)
-
-
-def write_kernel(
-    dims, table_ref, codes_ref, scale_ref, recv_ref, codes_out, scale_out, codes, scales, rem_code, rem_scale, rows, sems
-):
-    slots = dims[0]
+    lax.fori_loop(max(0, pairs - RING), pairs, drain, 0)
+
+    def edges(layer, carry):
+        @pl.when(part < parts_n - 1)
+        def _():
+            edge(layer, 0).wait_send()
+
+        @pl.when(part > 0)
+        def _():
+            edge(layer, 1).wait_send()
+
+        return carry
+
+    lax.fori_loop(0, layers, edges, 0)
+
+
+def write_kernel(group_ref, codes_ref, scale_ref, codes_out, scale_out, scales, sems):
     layers = codes_ref.shape[0]
-    done = layers - PAIR
-    pair = recv_ref.shape[1] - 1
     me = lax.axis_index("serve")
-    copies = [pltpu.make_async_copy(codes_ref.at[n], codes_out.at[n], sems.at[n]) for n in range(done)]
+    copies = [pltpu.make_async_copy(codes_ref.at[n], codes_out.at[n], sems.at[n]) for n in range(layers)]
     for copy in copies:
         copy.start()
-
-    def put_code(i, low, high, code):
-        codes[i // slots, i % slots, :, low:high] = code.astype(codes.dtype)
-
-    def mask(layer, k, scale):
-        return jnp.where(table_ref[layer, me * slots + k] > 0, scale, 0.0)
-
-    def put_scale(sub, k, scale):
-        scales[done + sub, k : k + 1, :] = mask(done + sub, k, scale)
-
-    unpack_pair(dims, lambda s, n: recv_ref[s, pair, n], rem_code, rem_scale, rows, put_code, put_scale)
-    tail = [
-        pltpu.make_async_copy(codes, codes_out.at[pl.ds(done, PAIR)], sems.at[done]),
-        pltpu.make_async_copy(scales, scale_out, sems.at[done + 1]),
-    ]
-    tail[0].start()
-
-    def masked(layer, carry):
-        for k in range(slots):
-            scales[layer, k : k + 1, :] = mask(layer, k, scale_ref[layer, k : k + 1, :])
-        return carry
-
-    lax.fori_loop(0, done, masked, 0)
-    tail[1].start()
-    for copy in copies + tail:
+    slot = lax.broadcasted_iota(jnp.int32, scales.shape[1:], 0)
+    for layer in range(layers):
+        count = jnp.sum(jnp.where(group_ref[layer : layer + 1, :] == me, 1, 0), axis=1, keepdims=True)
+        scales[layer] = jnp.where(slot < count, scale_ref[layer], 0.0)
+    copies.append(pltpu.make_async_copy(scales, scale_out, sems.at[layers]))
+    copies[-1].start()
+    for copy in copies:
         copy.wait()
 
 
@@ -369,34 +377,27 @@
     pieces = PAIR * slots * full + (1 if rem else 0)
     width = columns * serve_n
     dtype = train_weights.dtype
+    spots = -(-serve_n * slots // LANES) * LANES
     dims = (slots, full, rem, columns, serve_n)
     assert SHIFT == BLOCK and buffer_len % BLOCK == 0
     assert PAIR * slots * rem <= LANES and layers % PAIR == 0
 
-    position = jnp.arange(blocks_dev, dtype=jnp.int32)
-    earlier = position[None, :] < position[:, None]
     group_ids = block_group[:, :, 0]
-    same_group = group_ids[:, :, None] == group_ids[:, None, :]
-    order_in = jnp.sum((same_group & earlier[None]).astype(jnp.int32), axis=2)
-    place = group_ids * slots + order_in
-    slot_ids = jnp.arange(serve_n * slots, dtype=jnp.int32)
-    hit = place[:, None, :] == slot_ids[None, :, None]
-    table = jnp.sum(jnp.where(hit, position[None, None, :] + 1, 0), axis=2)
 
     smem = pl.BlockSpec(memory_space=pltpu.SMEM)
     vmem = pl.BlockSpec(memory_space=pltpu.VMEM)
     anywhere = pl.BlockSpec(memory_space=pl.ANY)
-    codes, scales, received = pl.pallas_call(
+    codes, scales = pl.pallas_call(
         functools.partial(move_kernel, dims),
-        in_specs=[smem, smem, anywhere],
-        out_specs=[vmem, vmem, vmem],
+        in_specs=[smem, vmem, anywhere],
+        out_specs=[vmem, vmem],
         out_shape=[
             pltpu.VMEM((layers, slots, BLOCK, width), dtype),
             pltpu.VMEM((layers, slots, width), jnp.float32),
-            pltpu.VMEM((serve_n, pairs, pieces, BLOCK, LANES), dtype),
         ],
         scratch_shapes=[
             pltpu.VMEM((serve_n, pairs, pieces, BLOCK, LANES), dtype),
+            pltpu.VMEM((serve_n, RING, pieces, BLOCK, LANES), dtype),
             pltpu.VMEM((PAIR, columns, buffer_len), dtype),
             pltpu.VMEM((buffer_len // BLOCK, BLOCK, columns), dtype),
             pltpu.VMEM((serve_n, PAIR * slots, BLOCK, LANES), dtype),
@@ -405,37 +406,36 @@
             pltpu.VMEM((serve_n, BLOCK, LANES), jnp.float32),
             pltpu.VMEM((serve_n, 1, LANES), jnp.float32),
             pltpu.VMEM((PAIR * slots, 1, width), jnp.float32),
+            pltpu.VMEM((layers, spots), jnp.int32),
+            pltpu.SMEM((layers, spots), jnp.int32),
             pltpu.SemaphoreType.DMA((PAIR,)),
-            pltpu.SemaphoreType.DMA((serve_n, pairs, PAIR)),
+            pltpu.SemaphoreType.DMA,
+            pltpu.SemaphoreType.DMA((serve_n, RING, PAIR)),
             pltpu.SemaphoreType.DMA((serve_n, pairs, PAIR)),
             pltpu.SemaphoreType.DMA((layers, 2)),
             pltpu.SemaphoreType.DMA((layers, 2)),
         ],
         compiler_params=pltpu.CompilerParams(
-            collective_id=0, has_side_effects=True, vmem_limit_bytes=26 * MIB
+            collective_id=0, has_side_effects=True, vmem_limit_bytes=36 * MIB
         ),
         name="move",
-    )(table, row_offset.T, jnp.swapaxes(train_weights, 1, 2))
+    )(row_offset.T, group_ids, jnp.swapaxes(train_weights, 1, 2))
 
     codes_out, scales_out = pl.pallas_call(
-        functools.partial(write_kernel, dims),
-        in_specs=[smem, vmem, vmem, vmem],
+        write_kernel,
+        in_specs=[vmem, anywhere, vmem],
         out_specs=[pl.BlockSpec(memory_space=pltpu.HBM)] * 2,
         out_shape=[
             jax.ShapeDtypeStruct((layers, slots, BLOCK, width), dtype),
             jax.ShapeDtypeStruct((layers, slots, width), jnp.float32),
         ],
         scratch_shapes=[
-            pltpu.VMEM((PAIR, slots, BLOCK, width), dtype),
             pltpu.VMEM((layers, slots, width), jnp.float32),
-            pltpu.VMEM((serve_n, BLOCK, LANES), jnp.float32),
-            pltpu.VMEM((serve_n, 1, LANES), jnp.float32),
-            pltpu.VMEM((PAIR * slots, 1, width), jnp.float32),
-            pltpu.SemaphoreType.DMA((layers,)),
+            pltpu.SemaphoreType.DMA((layers + 1,)),
         ],
-        compiler_params=pltpu.CompilerParams(vmem_limit_bytes=6 * MIB),
+        compiler_params=pltpu.CompilerParams(vmem_limit_bytes=2 * MIB),
         name="write",
-    )(table, codes, scales, received)
+    )(group_ids, codes, scales)
     return (
         codes_out.reshape(layers, 1, 1, slots, BLOCK, width),
         scales_out.reshape(layers, 1, 1, slots, width),

time: 223 us -> 208 us (0.933)
  local copies, waits for them, and re-layouts: 13.3 us -> 0.01 us
  other arithmetic: 2.81 us -> 0 us
    unnamed x6 -> x2, local copies, waits for them, and re-layouts: 13.3 us -> 0.01 us
where the time goes in v2:
time: 208 us
  Pallas kernels  207 us (100%)
    pallas_call x1, Pallas kernels, shards(): pl.pallas_call(functools.partial(move_kernel, dims), in_specs=[smem, vmem...  200 us
    pallas_call x1, Pallas kernels, shards(): pl.pallas_call(write_kernel, in_specs=[vmem, anywhere, vmem], out_specs=[...  6.63 us

profile of v2, /device:TPU:1, one launch (start us, length us, event | category | flops | bytes accessed | tf_op | source)
XLA Modules:
  0.0 207.7 jit_solution(4202023306271392077)
XLA Ops:
  0.6 0.0 copy-start
  0.6 200.4 %move.1 = (bf16[16,8,32,2112]{3,2,1,0:T(8,128)(2,1)S(1)}, f32[16,8,2112]{2,1,0:T(8,128)S(1)}) custom-call(s32[5,16]{1,0:T(8,128)} %bitcast.12, s32[16,56]{1,0:T(8,128)} %bitcast.9, bf16[16,264,1856]{2,1,0:T(8,128)(2,1)} %bitcast.11), custom_call_target="tpu_custom_call" | custom-call | tf_op jit(solution)/shard_map/move/pallas_call | solution.py:390
  201.1 0.0 copy-done
  201.1 6.6 %write.1 = (bf16[16,8,32,2112]{3,2,1,0:T(8,128)(2,1)}, f32[16,8,2112]{2,1,0:T(8,128)}) custom-call(s32[16,56]{1,0:T(8,128)S(1)} %bitcast.10, bf16[16,8,32,2112]{3,2,1,0:T(8,128)(2,1)S(1)} %get-tuple-element.6.codes_ref, f32[16,8,2112]{2,1,0:T(8,128)S(1)} %get-tuple-element.7.scale_ref), custom_call_target="tpu_custom_call" | custom-call | tf_op jit(solution)/shard_map/write/pallas_call | solution.py:424
Async XLA Ops:
  0.6 200.4 %copy-start = (s32[16,56,1]{1,2,0:T(1,128)S(1)}, s32[16,56,1]{1,2,0:T(1,128)}, u32[]{:S(2)}) copy-start(s32[16,56,1]{1,2,0:T(1,128)} %param.5) | copy-start | bytes 10756

commit v3 on v2

v3 whole, which is shorter than its diff:
```python
import functools

import jax
import jax.numpy as jnp
from jax import lax
from jax.experimental import pallas as pl
from jax.experimental.pallas import tpu as pltpu
from jax.sharding import PartitionSpec as P

BLOCK = 32
SHIFT = 32
LANES = 128
PAIR = 2
RING = 3
MESH = pl.DeviceIdType.MESH
MIB = 1024 * 1024


def turned(values):
    return jnp.transpose(values.astype(jnp.float32))


def partner(me, mask, count):
    out, bit = 0, 1
    while bit < count:
        out = out + ((me // bit + mask // bit) % 2) * bit
        bit *= 2
    return out


def scaled(values):
    values = values.astype(jnp.float32)
    divisor = jnp.maximum(jnp.max(jnp.abs(values), axis=0, keepdims=True), 0.25)
    return values * (1.0 / divisor), divisor


def scale_rest(dims, count, recv, rem_code, rem_scale):
    full, rem, columns, sources = dims
    if rem:
        for s in range(sources):
            rem_code[s], rem_scale[s] = scaled(recv(s, count * full))


def scale_slot(dims, i, recv, rem_code, rem_scale, put_code, put_scale):
    full, rem, columns, sources = dims
    width = columns * sources
    tiles = -(-width // LANES)
    lane = lax.broadcasted_iota(jnp.int32, (BLOCK, LANES), 1)
    lane_row = lax.broadcasted_iota(jnp.int32, (1, LANES), 1)
    parts = [None] * tiles

    def put(tile, low, code, scale):
        if tile >= tiles:
            return
        if parts[tile] is None:
            parts[tile] = (code, scale)
        else:
            before = parts[tile]
            parts[tile] = (jnp.where(lane >= low, code, before[0]), jnp.where(lane_row >= low, scale, before[1]))

    def flush(below):
        for tile in range(below):
            if parts[tile] is not None:
                code, scale = parts[tile]
                end = min(width, (tile + 1) * LANES)
                size = end - tile * LANES
                put_code(tile * LANES, end, code[:, :size])
                put_scale(tile * LANES, end, scale[:, :size])
                parts[tile] = None

    for s in range(sources):
        for t in range(full + (1 if rem else 0)):
            start = s * columns + t * LANES
            size = LANES if t < full else rem
            low = start % LANES
            if t < full:
                code, scale = scaled(recv(s, i * full + t))
                if low:
                    code, scale = pltpu.roll(code, low, 1), pltpu.roll(scale, low, 1)
            else:
                turn = lax.rem(low + LANES - i * rem, LANES)
                code, scale = pltpu.roll(rem_code[s], turn, 1), pltpu.roll(rem_scale[s], turn, 1)
            tile = start // LANES
            put(tile, low, code, scale)
            if low + size > LANES:
                put(tile + 1, 0, code, scale)
            flush((start + size) // LANES)
    flush(tiles)


def move_kernel(
    dims,
    base,
    offset_ref,
    group_ref,
    wt_ref,
    codes_ref,
    scale_ref,
    first_ref,
    second_ref,
    longest_ref,
    recv_ref,
    send_ref,
    in_ref,
    w_ref,
    rem_ref,
    edge_ref,
    halo_ref,
    over_ref,
    list_ref,
    rem_code,
    rem_scale,
    rows,
    table_ref,
    table_smem,
    length_ref,
    lengths_ref,
    in_sem,
    table_sem,
    send_sem,
    recv_sem,
    halo_send,
    halo_recv,
    list_send,
    list_recv,
    length_send,
    length_recv,
    second_sem,
):
    full, rem, columns, groups = dims
    slots = base + 1
    pairs = recv_ref.shape[1]
    layers = pairs * PAIR
    listed = layers // 2
    blocks = w_ref.shape[0]
    buffer_len = blocks * BLOCK
    rows_dev = buffer_len - 2 * SHIFT
    me = lax.axis_index("serve")
    part = lax.axis_index("train")
    parts_n = lax.axis_size("train")
    half = base * full
    rest = half + (1 if rem else 0)

    def fetch(layer, sub):
        return pltpu.make_async_copy(wt_ref.at[layer], in_ref.at[sub], in_sem.at[sub])

    def message(mask, pair, sub):
        peer = partner(me, mask, groups)
        span = pl.ds(sub * half, rest if sub == PAIR - 1 else half)
        return pltpu.make_async_remote_copy(
            send_ref.at[peer, pair % RING, span],
            recv_ref.at[me, pair, span],
            send_sem.at[mask, pair % RING, sub],
            recv_sem.at[mask, pair, sub],
            device_id={"serve": peer},
            device_id_type=MESH,
        )

    def arrival(mask, pair, sub):
        peer = partner(me, mask, groups)
        span = pl.ds(sub * half, rest if sub == PAIR - 1 else half)
        return pltpu.make_async_remote_copy(
            recv_ref.at[peer, pair, span],
            recv_ref.at[peer, pair, span],
            send_sem.at[mask, pair % RING, sub],
            recv_sem.at[mask, pair, sub],
            device_id={"serve": peer},
            device_id_type=MESH,
        )

    def list_message(mask):
        peer = partner(me, mask, groups)
        return pltpu.make_async_remote_copy(
            list_ref.at[0, peer],
            first_ref.at[me],
            list_send.at[mask],
            list_recv.at[mask],
            device_id={"serve": peer},
            device_id_type=MESH,
        )

    def edge(layer, side):
        to = part + 1 if side == 0 else part - 1
        return pltpu.make_async_remote_copy(
            edge_ref.at[layer, side],
            halo_ref.at[layer, side],
            halo_send.at[layer, side],
            halo_recv.at[layer, side],
            device_id={"train": to},
            device_id_type=MESH,
        )

    def length_message(ahead):
        return pltpu.make_async_remote_copy(
            length_ref,
            lengths_ref.at[ahead],
            length_send.at[ahead],
            length_recv.at[ahead],
            device_id={"train": (part + ahead) % parts_n},
            device_id_type=MESH,
        )

    for sub in range(PAIR):
        fetch(sub, sub).start()

    barrier = pltpu.get_barrier_semaphore()

    def greet(mask, carry):
        pl.semaphore_signal(barrier, inc=1, device_id={"serve": partner(me, mask, groups)}, device_id_type=MESH)
        return carry

    lax.fori_loop(1, groups, greet, 0)
    for ahead in range(1, parts_n):
        pl.semaphore_signal(barrier, inc=1, device_id={"train": (part + ahead) % parts_n}, device_id_type=MESH)

    spot = lax.broadcasted_iota(jnp.int32, (layers, groups * layers), 1)
    spot_group = jnp.zeros(spot.shape, jnp.int32)
    for g in range(1, groups):
        spot_group = spot_group + jnp.where(spot >= g * layers, 1, 0)
    spot_slot = spot - spot_group * layers
    seen = jnp.zeros(spot.shape, jnp.int32)
    table = jnp.zeros(spot.shape, jnp.int32)
    for j in range(group_ref.shape[1]):
        mine = group_ref[:, j : j + 1] == spot_group
        table = jnp.where(mine & (seen == spot_slot), j + 1, table)
        seen = jnp.where(mine, seen + 1, seen)
    table_ref[0:layers, :] = table
    length = jnp.zeros((1, groups * layers), jnp.int32)
    entry = jnp.full((1, groups * layers), layers, jnp.int32)
    for n in range(layers):
        long = seen[n : n + 1, :] == slots
        entry = jnp.where(long & (length == spot_slot[0:1, :]), n, entry)
        length = jnp.where(long, length + 1, length)
    table_ref[layers : layers + 1, :] = entry
    to_smem = pltpu.make_async_copy(table_ref, table_smem, table_sem)
    to_smem.start()
    most = jnp.max(length.astype(jnp.float32), axis=1, keepdims=True)
    length_ref[...] = jnp.broadcast_to(most, length_ref.shape)
    over_ref[:, layers] = jnp.zeros((groups, BLOCK, columns), over_ref.dtype)
    to_smem.wait()
    pl.semaphore_wait(barrier, groups - 1 + parts_n - 1)

    row = lax.broadcasted_iota(jnp.int32, (BLOCK, columns), 0)
    lane = lax.broadcasted_iota(jnp.int32, (BLOCK, LANES), 1)
    last = rows_dev - BLOCK

    def transpose_tile(sub, low):
        high = min(low + LANES, buffer_len)
        rows_of = turned(in_ref[sub, :, low:high]).astype(w_ref.dtype)
        w_ref[low // BLOCK : high // BLOCK] = rows_of.reshape((high - low) // BLOCK, BLOCK, columns)

    def joined(group, count):
        tile = rem_ref[group, 0].astype(jnp.float32)
        for i in range(1, count):
            moved = pltpu.roll(rem_ref[group, i].astype(jnp.float32), i * rem, 1)
            tile = jnp.where(lane >= i * rem, moved, tile)
        return tile

    def pack_layer(pair, sub):
        layer = pair * PAIR + sub
        fetch(layer, sub).wait()
        lows = list(range(0, buffer_len, LANES))
        lows = [lows[0], lows[-1]] + lows[1:-1]
        for low in lows[:2]:
            transpose_tile(sub, low)
        edge_ref[layer, 0] = w_ref[blocks - 1]
        edge_ref[layer, 1] = w_ref[0]

        @pl.when(part < parts_n - 1)
        def _():
            edge(layer, 0).start()

        @pl.when(part > 0)
        def _():
            edge(layer, 1).start()

        for low in lows[2:]:
            transpose_tile(sub, low)

        @pl.when(layer + PAIR < layers)
        def _():
            fetch(layer + PAIR, sub).start()

        base_row = part * rows_dev

        @pl.when(part > 0)
        def _():
            edge(layer, 0).wait_recv()
            first = offset_ref[part, layer] - base_row
            head = jnp.where(row < first, halo_ref[layer, 0].astype(jnp.float32), w_ref[1].astype(jnp.float32))
            w_ref[1] = head.astype(w_ref.dtype)

        @pl.when(part < parts_n - 1)
        def _():
            edge(layer, 1).wait_recv()
            after = offset_ref[part + 1, layer] - base_row
            tail = w_ref[blocks - 2].astype(jnp.float32)
            tail = jnp.where(row + last >= after, halo_ref[layer, 1].astype(jnp.float32), tail)
            w_ref[blocks - 2] = tail.astype(w_ref.dtype)

        w_ref[0] = jnp.zeros((BLOCK, columns), w_ref.dtype)

        def gather(group, out):
            for k in range(base):
                block = w_ref[table_smem[layer, group * layers + k]]
                for t in range(full):
                    out[(sub * base + k) * full + t] = block[:, t * LANES : (t + 1) * LANES]
                if rem:
                    rem_ref[group, sub * base + k, :, 0:rem] = block[:, full * LANES :]
            over_ref[group, layer] = w_ref[table_smem[layer, group * layers + base]]
            if rem and sub == PAIR - 1:
                out[PAIR * half] = joined(group, PAIR * base).astype(out.dtype)

        def give(mask, carry):
            peer = partner(me, mask, groups)
            gather(peer, send_ref.at[peer, pair % RING])
            message(mask, pair, sub).start()
            return carry

        lax.fori_loop(2, groups, give, 0)
        give(1, 0)
        gather(me, recv_ref.at[me, pair])

    def pack_list(group, which, out):
        for e in range(listed):
            block = over_ref[group, table_smem[layers, group * layers + which * listed + e]]
            for t in range(full):
                out[e * full + t] = block[:, t * LANES : (t + 1) * LANES]
            if rem:
                rem_ref[group, e, :, 0:rem] = block[:, full * LANES :]
        if rem:
            out[listed * full] = joined(group, listed).astype(out.dtype)

    def take(pair):
        for sub in range(PAIR):

            def arrive(mask, carry, sub=sub):
                arrival(mask, pair, sub).wait_recv()
                return carry

            lax.fori_loop(1, groups, arrive, 0)

    def unpack(pair):
        def recv(s, n):
            return recv_ref[s, pair, n]

        scale_rest(dims, PAIR * base, recv, rem_code, rem_scale)

        def slot(i, carry):
            def put_code(low, high, code):
                codes_ref[pair * PAIR + i // base, i % base, :, low:high] = code.astype(codes_ref.dtype)

            def put_scale(low, high, scale):
                rows[i, :, low:high] = scale

            scale_slot(dims, i, recv, rem_code, rem_scale, put_code, put_scale)
            return carry

        lax.fori_loop(0, PAIR * base, slot, 0)
        for i in range(PAIR * base):
            scale_ref[pair * PAIR + i // base, i % base : i % base + 1, :] = rows[i]

    def sent(pair):
        for sub in range(PAIR):

            def leave(mask, carry, sub=sub):
                message(mask, pair, sub).wait_send()
                return carry

            lax.fori_loop(1, groups, leave, 0)

    def step(pair, carry):
        @pl.when(pair >= RING)
        def _():
            sent(pair - RING)

        for sub in range(PAIR):
            pack_layer(pair, sub)

        @pl.when(pair > 0)
        def _():
            take(pair - 1)
            unpack(pair - 1)

        return carry

    for ahead in range(1, parts_n):
        length_message(ahead).start()
    lax.fori_loop(0, pairs, step, 0)

    def give_list(mask, carry):
        peer = partner(me, mask, groups)
        pack_list(peer, 0, list_ref.at[0, peer])
        list_message(mask).start()
        return carry

    lax.fori_loop(1, groups, give_list, 0)
    pack_list(me, 0, first_ref.at[me])

    def second(group, carry):
        pack_list(group, 1, list_ref.at[1, group])
        return carry

    lax.fori_loop(0, groups, second, 0)
    keep = pltpu.make_async_copy(list_ref.at[1], second_ref, second_sem)
    keep.start()
    for ahead in range(1, parts_n):
        length_message(ahead).wait()
        most = jnp.maximum(most, lengths_ref[ahead, 0:1, 0:1])
    longest_ref[0, 0] = jnp.max(most).astype(jnp.int32)

    take(pairs - 1)
    unpack(pairs - 1)

    def drain(pair, carry):
        sent(pair)
        return carry

    lax.fori_loop(max(0, pairs - RING), pairs, drain, 0)

    def edges(layer, carry):
        @pl.when(part < parts_n - 1)
        def _():
            edge(layer, 0).wait_send()

        @pl.when(part > 0)
        def _():
            edge(layer, 1).wait_send()

        return carry

    lax.fori_loop(0, layers, edges, 0)
    keep.wait()

    def listed_all(mask, carry):
        list_message(mask).wait()
        return carry

    lax.fori_loop(1, groups, listed_all, 0)


def list_places(group_ref, place_ref, slots):
    layers = group_ref.shape[0]
    me = lax.axis_index("serve")
    count = jnp.sum(jnp.where(group_ref[...] == me, 1, 0), axis=1, keepdims=True)
    length = jnp.zeros((1, 1), jnp.int32)
    for n in range(layers):
        long = count[n : n + 1, :] == slots
        place_ref[n : n + 1, :] = jnp.broadcast_to(jnp.where(long, length, layers), (1, place_ref.shape[1]))
        length = jnp.where(long, length + 1, length)
    return count


def write_kernel(
    dims,
    base,
    group_ref,
    codes_ref,
    scale_ref,
    first_ref,
    codes_out,
    scale_out,
    scales,
    extra,
    extra_scale,
    rem_code,
    rem_scale,
    place_ref,
    place_smem,
    sems,
    extra_sems,
    place_sem,
):
    full, rem, columns, groups = dims
    layers = codes_ref.shape[0]
    listed = layers // 2
    copies = [
        pltpu.make_async_copy(codes_ref.at[n], codes_out.at[n, pl.ds(0, base)], sems.at[n]) for n in range(layers)
    ]
    for copy in copies:
        copy.start()
    count = list_places(group_ref, place_ref, base + 1)
    to_smem = pltpu.make_async_copy(place_ref, place_smem, place_sem)
    to_smem.start()
    extra[layers] = jnp.zeros(extra.shape[1:], extra.dtype)

    def recv(s, n):
        return first_ref[s, n]

    scale_rest(dims, listed, recv, rem_code, rem_scale)
    slot = lax.broadcasted_iota(jnp.int32, scales.shape[1:], 0)
    to_smem.wait()

    def last_slot(layer, carry):
        place = place_smem[layer, 0]
        long = place < layers
        extra_scale[layer] = jnp.zeros(extra_scale.shape[1:], jnp.float32)

        @pl.when(long)
        def _():
            def put_code(low, high, code):
                extra[layer, :, low:high] = code.astype(extra.dtype)

            def put_scale(low, high, scale):
                extra_scale[layer, :, low:high] = scale

            scale_slot(dims, jnp.minimum(place, listed - 1), recv, rem_code, rem_scale, put_code, put_scale)

        pltpu.make_async_copy(
            extra.at[jnp.where(long, layer, layers)], codes_out.at[layer, base], extra_sems.at[layer]
        ).start()
        return carry

    lax.fori_loop(0, layers, last_slot, 0)
    for n in range(layers):
        own = jnp.where(slot < count[n : n + 1, :], scale_ref[n], 0.0)
        scales[n] = jnp.where(slot < base, own, jnp.broadcast_to(extra_scale[n], own.shape))
    copies.append(pltpu.make_async_copy(scales, scale_out, sems.at[layers]))
    copies[-1].start()
    for n in range(layers):
        copies.append(pltpu.make_async_copy(extra.at[n], codes_out.at[n, base], extra_sems.at[n]))
    for copy in copies:
        copy.wait()


def late_kernel(
    dims,
    base,
    group_ref,
    got_ref,
    codes_in,
    scale_in,
    codes_out,
    scale_out,
    extra,
    extra_scale,
    scales,
    rem_code,
    rem_scale,
    place_ref,
    place_smem,
    sem,
):
    del codes_in, scale_in
    full, rem, columns, groups = dims
    layers = codes_out.shape[0]
    listed = layers // 2
    list_places(group_ref, place_ref, base + 1)
    to_smem = pltpu.make_async_copy(place_ref, place_smem, sem)
    to_smem.start()
    to_smem.wait()

    def recv(s, n):
        return got_ref[s, n]

    scale_rest(dims, listed, recv, rem_code, rem_scale)
    slot = lax.broadcasted_iota(jnp.int32, scales.shape, 0)

    def last_slot(layer, carry):
        place = place_smem[layer, 0]

        @pl.when((place >= listed) & (place < layers))
        def _():
            def put_code(low, high, code):
                extra[:, low:high] = code.astype(extra.dtype)

            def put_scale(low, high, scale):
                extra_scale[:, low:high] = scale

            scale_slot(dims, place - listed, recv, rem_code, rem_scale, put_code, put_scale)
            pltpu.sync_copy(extra, codes_out.at[layer, base])
            pltpu.sync_copy(scale_out.at[layer], scales)
            scales[...] = jnp.where(slot < base, scales[...], jnp.broadcast_to(extra_scale[...], scales.shape))
            pltpu.sync_copy(scales, scale_out.at[layer])

        return carry

    lax.fori_loop(0, layers, last_slot, 0)


def shards(train_weights, row_offset, block_group):
    train_n = lax.axis_size("train")
    serve_n = lax.axis_size("serve")
    layers, buffer_len, columns = train_weights.shape
    blocks_dev = block_group.shape[1]
    base = (blocks_dev + serve_n - 1) // serve_n
    slots = base + 1
    full = columns // LANES
    rem = columns - full * LANES
    pairs = layers // PAIR
    listed = layers // 2
    pieces = PAIR * base * full + (1 if rem else 0)
    pieces_list = listed * full + (1 if rem else 0)
    rests = max(PAIR * base, listed)
    spots = serve_n * layers
    width = columns * serve_n
    dtype = train_weights.dtype
    dims = (full, rem, columns, serve_n)
    assert SHIFT == BLOCK and buffer_len % BLOCK == 0
    assert rests * rem <= LANES and layers % PAIR == 0 and slots <= layers

    group_ids = block_group[:, :, 0]
    smem = pl.BlockSpec(memory_space=pltpu.SMEM)
    vmem = pl.BlockSpec(memory_space=pltpu.VMEM)
    anywhere = pl.BlockSpec(memory_space=pl.ANY)
    codes, scales, first, second, longest = pl.pallas_call(
        functools.partial(move_kernel, dims, base),
        in_specs=[smem, vmem, anywhere],
        out_specs=[vmem, vmem, vmem, pl.BlockSpec(memory_space=pltpu.HBM), smem],
        out_shape=[
            pltpu.VMEM((layers, base, BLOCK, width), dtype),
            pltpu.VMEM((layers, slots, width), jnp.float32),
            pltpu.VMEM((serve_n, pieces_list, BLOCK, LANES), dtype),
            jax.ShapeDtypeStruct((serve_n, pieces_list, BLOCK, LANES), dtype),
            jax.ShapeDtypeStruct((1, 1), jnp.int32),
        ],
        scratch_shapes=[
            pltpu.VMEM((serve_n, pairs, pieces, BLOCK, LANES), dtype),
            pltpu.VMEM((serve_n, RING, pieces, BLOCK, LANES), dtype),
            pltpu.VMEM((PAIR, columns, buffer_len), dtype),
            pltpu.VMEM((buffer_len // BLOCK, BLOCK, columns), dtype),
            pltpu.VMEM((serve_n, rests, BLOCK, LANES), dtype),
            pltpu.VMEM((layers, 2, SHIFT, columns), dtype),
            pltpu.VMEM((layers, 2, SHIFT, columns), dtype),
            pltpu.VMEM((serve_n, layers + 1, BLOCK, columns), dtype),
            pltpu.VMEM((2, serve_n, pieces_list, BLOCK, LANES), dtype),
            pltpu.VMEM((serve_n, BLOCK, LANES), jnp.float32),
            pltpu.VMEM((serve_n, 1, LANES), jnp.float32),
            pltpu.VMEM((PAIR * base, 1, width), jnp.float32),
            pltpu.VMEM((layers + 8, spots), jnp.int32),
            pltpu.SMEM((layers + 8, spots), jnp.int32),
            pltpu.VMEM((8, LANES), jnp.float32),
            pltpu.VMEM((train_n, 8, LANES), jnp.float32),
            pltpu.SemaphoreType.DMA((PAIR,)),
            pltpu.SemaphoreType.DMA,
            pltpu.SemaphoreType.DMA((serve_n, RING, PAIR)),
            pltpu.SemaphoreType.DMA((serve_n, pairs, PAIR)),
            pltpu.SemaphoreType.DMA((layers, 2)),
            pltpu.SemaphoreType.DMA((layers, 2)),
            pltpu.SemaphoreType.DMA((serve_n,)),
            pltpu.SemaphoreType.DMA((serve_n,)),
            pltpu.SemaphoreType.DMA((train_n,)),
            pltpu.SemaphoreType.DMA((train_n,)),
            pltpu.SemaphoreType.DMA,
        ],
        compiler_params=pltpu.CompilerParams(
            collective_id=0, has_side_effects=True, vmem_limit_bytes=36 * MIB
        ),
        name="move",
    )(row_offset.T, group_ids, jnp.swapaxes(train_weights, 1, 2))

    codes_shape = jax.ShapeDtypeStruct((layers, slots, BLOCK, width), dtype)
    scales_shape = jax.ShapeDtypeStruct((layers, slots, width), jnp.float32)
    hbm = pl.BlockSpec(memory_space=pltpu.HBM)
    rest_scratch = [
        pltpu.VMEM((serve_n, BLOCK, LANES), jnp.float32),
        pltpu.VMEM((serve_n, 1, LANES), jnp.float32),
        pltpu.VMEM((layers, LANES), jnp.int32),
        pltpu.SMEM((layers, LANES), jnp.int32),
    ]
    codes_out, scales_out = pl.pallas_call(
        functools.partial(write_kernel, dims, base),
        in_specs=[vmem, anywhere, vmem, vmem],
        out_specs=[hbm, hbm],
        out_shape=[codes_shape, scales_shape],
        scratch_shapes=[
            pltpu.VMEM((layers, slots, width), jnp.float32),
            pltpu.VMEM((layers + 1, BLOCK, width), dtype),
            pltpu.VMEM((layers, 1, width), jnp.float32),
            *rest_scratch,
            pltpu.SemaphoreType.DMA((layers + 1,)),
            pltpu.SemaphoreType.DMA((layers,)),
            pltpu.SemaphoreType.DMA,
        ],
        compiler_params=pltpu.CompilerParams(vmem_limit_bytes=6 * MIB),
        name="write",
    )(group_ids, codes, scales, first)

    def late(state):
        got = lax.all_to_all(second, "serve", split_axis=0, concat_axis=0, tiled=True)
        late_codes, late_scales = pl.pallas_call(
            functools.partial(late_kernel, dims, base),
            in_specs=[vmem, vmem, hbm, hbm],
            out_specs=[hbm, hbm],
            out_shape=[codes_shape, scales_shape],
            input_output_aliases={2: 0, 3: 1},
            scratch_shapes=[
                pltpu.VMEM((BLOCK, width), dtype),
                pltpu.VMEM((1, width), jnp.float32),
                pltpu.VMEM((slots, width), jnp.float32),
                *rest_scratch,
                pltpu.SemaphoreType.DMA,
            ],
            compiler_params=pltpu.CompilerParams(vmem_limit_bytes=6 * MIB),
            name="late",
        )(group_ids, got, state[1], state[2])
        return jnp.zeros((), jnp.int32), late_codes, late_scales

    state = (longest[0, 0], codes_out, scales_out)
    _, codes_out, scales_out = lax.while_loop(lambda now: now[0] > listed, late, state)
    return (
        codes_out.reshape(layers, 1, 1, slots, BLOCK, width),
        scales_out.reshape(layers, 1, 1, slots, width),
    )


def solution(mesh):
    return jax.shard_map(
        shards,
        mesh=mesh,
        in_specs=(P(None, "train", "serve"), P(), P(None, "train", None)),
        out_specs=(
            P(None, "serve", "train", None, None, None),
            P(None, "serve", "train", None, None),
        ),
        check_vma=False,
    )
```

time: 208 us -> 198 us (0.952)
  Pallas kernels: 207 us -> 195 us
    pallas_call x2, Pallas kernels: 207 us -> 195 us  [the longest x1 188 us: shards(): pl.pallas_call(functools.partial(move_kernel, dims, base), in_specs=[smem...]
where the time goes in v3:
time: 198 us
  Pallas kernels  195 us (98%)
    pallas_call x1, Pallas kernels, shards(): pl.pallas_call(functools.partial(move_kernel, dims, base), in_specs=[smem...  188 us
    pallas_call x1, Pallas kernels, shards(): pl.pallas_call(functools.partial(write_kernel, dims, base), in_specs=[vme...  6.42 us

profile of v3, /device:TPU:1, one launch (start us, length us, event | category | flops | bytes accessed | tf_op | source)
XLA Modules:
  0.0 197.6 jit_solution(16941756921041132179)
XLA Ops:
  0.6 0.0 copy-start
  0.6 0.7 copy-done
  1.3 0.0 copy-start.2
  1.3 188.1 %move.1 = (bf16[16,7,32,2112]{3,2,1,0:T(8,128)(2,1)S(1)}, f32[16,8,2112]{2,1,0:T(8,128)S(1)}, bf16[8,17,32,128]{3,2,1,0:T(8,128)(2,1)S(1)}, bf16[8,17,32,128]{3,2,1,0:T(8,128)(2,1)}, s32[1,1]{1,0:T(1,128)}) custom-call(s32[5,16]{1,0:T(8,128)S(1)} %bitcast.6, s32[16,56]{1,0:T(8,128)} %bitcast.10, bf16[16,264,1856]{2,1,0:T(8,128)(2,1)} %bitcast.9), custom_call_target="tpu_custom_call" | custom-call | tf_op jit(solution)/shard_map/move/pallas_call | solution.py:606
  189.5 0.0 copy-done.2
  189.5 6.4 %write.1 = (bf16[16,8,32,2112]{3,2,1,0:T(8,128)(2,1)}, f32[16,8,2112]{2,1,0:T(8,128)S(1)}) custom-call(s32[16,56]{1,0:T(8,128)S(1)} %bitcast.11, bf16[16,7,32,2112]{3,2,1,0:T(8,128)(2,1)S(1)} %get-tuple-element.39.codes_ref, f32[16,8,2112]{2,1,0:T(8,128)S(1)} %get-tuple-element.40.scale_ref, bf16[8,17,32,128]{3,2,1,0:T(8,128)(2,1)S(1)} %get-tuple-element.41.first_ref), custom_call_target="tpu_custom_call" | custom-call | tf_op jit(solution)/shard_map/write/pallas_call | solution.py:661
  195.9 0.7 while.11
  196.6 0.0 copy-start.1
  196.6 1.0 copy-done.1
Async XLA Ops:
  0.6 0.7 copy-start
  1.3 188.1 %copy-start.2 = (s32[16,56,1]{1,2,0:T(1,128)S(1)}, s32[16,56,1]{1,2,0:T(1,128)}, u32[]{:S(2)}) copy-start(s32[16,56,1]{1,2,0:T(1,128)} %param.7) | copy-start | bytes 10756
  196.6 1.0 copy-start.1

commit v4 on v3

--- a/solution.py
+++ b/solution.py
@@ -91,12 +91,13 @@
 def move_kernel(
     dims,
     base,
-    offset_ref,
-    group_ref,
+    offset_hbm,
+    group_hbm,
     wt_ref,
     codes_ref,
     scale_ref,
-    first_ref,
+    tail_ref,
+    all_ref,
     second_ref,
     longest_ref,
     recv_ref,
@@ -115,8 +116,11 @@
     table_smem,
     length_ref,
     lengths_ref,
+    offset_ref,
+    group_ref,
     in_sem,
     table_sem,
+    small_sem,
     send_sem,
     recv_sem,
     halo_send,
@@ -129,7 +133,7 @@
 ):
     full, rem, columns, groups = dims
     slots = base + 1
-    pairs = recv_ref.shape[1]
+    pairs = recv_ref.shape[1] + 1
     layers = pairs * PAIR
     listed = layers // 2
     blocks = w_ref.shape[0]
@@ -144,38 +148,63 @@
     def fetch(layer, sub):
         return pltpu.make_async_copy(wt_ref.at[layer], in_ref.at[sub], in_sem.at[sub])
 
-    def message(mask, pair, sub):
+    def message(mask, pair, sub, final):
         peer = partner(me, mask, groups)
         span = pl.ds(sub * half, rest if sub == PAIR - 1 else half)
         return pltpu.make_async_remote_copy(
             send_ref.at[peer, pair % RING, span],
-            recv_ref.at[me, pair, span],
+            tail_ref.at[me, span] if final else recv_ref.at[me, pair, span],
             send_sem.at[mask, pair % RING, sub],
             recv_sem.at[mask, pair, sub],
             device_id={"serve": peer},
             device_id_type=MESH,
         )
 
-    def arrival(mask, pair, sub):
+    def arrival(mask, pair, sub, final):
         peer = partner(me, mask, groups)
         span = pl.ds(sub * half, rest if sub == PAIR - 1 else half)
+        place = tail_ref.at[peer, span] if final else recv_ref.at[peer, pair, span]
         return pltpu.make_async_remote_copy(
-            recv_ref.at[peer, pair, span],
-            recv_ref.at[peer, pair, span],
+            place,
+            place,
             send_sem.at[mask, pair % RING, sub],
             recv_sem.at[mask, pair, sub],
             device_id={"serve": peer},
             device_id_type=MESH,
         )
 
-    def list_message(mask):
-        peer = partner(me, mask, groups)
+    bits = [1 << n for n in range(groups.bit_length() - 1)]
+    orders = [bits[1:] + bits[:1], bits[:0:-1] + bits[:1]]
+    pieces_list = all_ref.shape[1]
+    spans = [pl.ds(0, pieces_list // 2), pl.ds(pieces_list // 2, pieces_list - pieces_list // 2)]
+
+    def stage(number):
+        for which, order in enumerate(orders):
+            held = [0]
+            for bit in order[:number]:
+                held = held + [mask + bit for mask in held]
+            for mask in held:
+                yield which, order[number], mask
+
+    def list_message(which, bit, mask):
+        place = all_ref.at[partner(me, mask, groups), spans[which]]
         return pltpu.make_async_remote_copy(
-            list_ref.at[0, peer],
-            first_ref.at[me],
-            list_send.at[mask],
-            list_recv.at[mask],
-            device_id={"serve": peer},
+            place,
+            place,
+            list_send.at[which, bit + mask],
+            list_recv.at[which, bit + mask],
+            device_id={"serve": partner(me, bit, groups)},
+            device_id_type=MESH,
+        )
+
+    def list_arrival(which, bit, mask):
+        place = all_ref.at[partner(me, bit + mask, groups), spans[which]]
+        return pltpu.make_async_remote_copy(
+            place,
+            place,
+            list_send.at[which, bit + mask],
+            list_recv.at[which, bit + mask],
+            device_id={"serve": partner(me, bit, groups)},
             device_id_type=MESH,
         )
 
@@ -200,7 +229,12 @@
             device_id_type=MESH,
         )
 
-    for sub in range(PAIR):
+    get_group = pltpu.make_async_copy(group_hbm, group_ref, small_sem.at[0])
+    get_group.start()
+    fetch(0, 0).start()
+    get_offset = pltpu.make_async_copy(offset_hbm, offset_ref, small_sem.at[1])
+    get_offset.start()
+    for sub in range(1, PAIR):
         fetch(sub, sub).start()
 
     barrier = pltpu.get_barrier_semaphore()
@@ -213,6 +247,7 @@
     for ahead in range(1, parts_n):
         pl.semaphore_signal(barrier, inc=1, device_id={"train": (part + ahead) % parts_n}, device_id_type=MESH)
 
+    get_group.wait()
     spot = lax.broadcasted_iota(jnp.int32, (layers, groups * layers), 1)
     spot_group = jnp.zeros(spot.shape, jnp.int32)
     for g in range(1, groups):
@@ -225,18 +260,29 @@
         table = jnp.where(mine & (seen == spot_slot), j + 1, table)
         seen = jnp.where(mine, seen + 1, seen)
     table_ref[0:layers, :] = table
+    none = layers * groups
     length = jnp.zeros((1, groups * layers), jnp.int32)
-    entry = jnp.full((1, groups * layers), layers, jnp.int32)
+    entry = jnp.full(length.shape, none, jnp.int32)
+    total = jnp.zeros((1, LANES), jnp.int32)
+    shared = jnp.full(total.shape, none, jnp.int32)
+    number = lax.broadcasted_iota(jnp.int32, total.shape, 1)
+    long = jnp.where(seen == slots, 1, 0)
     for n in range(layers):
-        long = seen[n : n + 1, :] == slots
-        entry = jnp.where(long & (length == spot_slot[0:1, :]), n, entry)
-        length = jnp.where(long, length + 1, length)
+        here = long[n : n + 1, :]
+        entry = jnp.where((here > 0) & (length == spot_slot[0:1, :]), n * groups + spot_group[0:1, :], entry)
+        length = length + here
+        for g in range(groups):
+            one = jnp.broadcast_to(here[:, g * layers : g * layers + 1], total.shape)
+            shared = jnp.where((one > 0) & (total == number), n * groups + g, shared)
+            total = total + one
     table_ref[layers : layers + 1, :] = entry
+    table_ref[layers + 1 : layers + 2, 0:LANES] = shared
     to_smem = pltpu.make_async_copy(table_ref, table_smem, table_sem)
     to_smem.start()
-    most = jnp.max(length.astype(jnp.float32), axis=1, keepdims=True)
+    most = total.astype(jnp.float32)
     length_ref[...] = jnp.broadcast_to(most, length_ref.shape)
-    over_ref[:, layers] = jnp.zeros((groups, BLOCK, columns), over_ref.dtype)
+    over_ref[none] = jnp.zeros((BLOCK, columns), over_ref.dtype)
+    get_offset.wait()
     to_smem.wait()
     pl.semaphore_wait(barrier, groups - 1 + parts_n - 1)
 
@@ -256,7 +302,7 @@
             tile = jnp.where(lane >= i * rem, moved, tile)
         return tile
 
-    def pack_layer(pair, sub):
+    def prepare(pair, sub):
         layer = pair * PAIR + sub
         fetch(layer, sub).wait()
         lows = list(range(0, buffer_len, LANES))
@@ -300,42 +346,49 @@
 
         w_ref[0] = jnp.zeros((BLOCK, columns), w_ref.dtype)
 
-        def gather(group, out):
-            for k in range(base):
-                block = w_ref[table_smem[layer, group * layers + k]]
-                for t in range(full):
-                    out[(sub * base + k) * full + t] = block[:, t * LANES : (t + 1) * LANES]
-                if rem:
-                    rem_ref[group, sub * base + k, :, 0:rem] = block[:, full * LANES :]
-            over_ref[group, layer] = w_ref[table_smem[layer, group * layers + base]]
-            if rem and sub == PAIR - 1:
-                out[PAIR * half] = joined(group, PAIR * base).astype(out.dtype)
-
-        def give(mask, carry):
+        def last_slots(group, carry):
+            over_ref[layer * groups + group] = w_ref[table_smem[layer, group * layers + base]]
+            return carry
+
+        lax.fori_loop(0, groups, last_slots, 0)
+
+    def gather(pair, sub, group, out):
+        for k in range(base):
+            block = w_ref[table_smem[pair * PAIR + sub, group * layers + k]]
+            for t in range(full):
+                out[(sub * base + k) * full + t] = block[:, t * LANES : (t + 1) * LANES]
+            if rem:
+                rem_ref[group, sub * base + k, :, 0:rem] = block[:, full * LANES :]
+        if rem and sub == PAIR - 1:
+            out[PAIR * half] = joined(group, PAIR * base).astype(out.dtype)
+
+    def give(low, high, pair, sub, final):
+        def one(mask, carry):
             peer = partner(me, mask, groups)
-            gather(peer, send_ref.at[peer, pair % RING])
-            message(mask, pair, sub).start()
+            gather(pair, sub, peer, send_ref.at[peer, pair % RING])
+            message(mask, pair, sub, final).start()
             return carry
 
-        lax.fori_loop(2, groups, give, 0)
-        give(1, 0)
-        gather(me, recv_ref.at[me, pair])
-
-    def pack_list(group, which, out):
+        lax.fori_loop(low, high, one, 0)
+
+    def own(pair, sub, final):
+        gather(pair, sub, me, tail_ref.at[me] if final else recv_ref.at[me, pair])
+
+    def pack_list(entry_of, out):
         for e in range(listed):
-            block = over_ref[group, table_smem[layers, group * layers + which * listed + e]]
+            block = over_ref[entry_of(e)]
             for t in range(full):
                 out[e * full + t] = block[:, t * LANES : (t + 1) * LANES]
             if rem:
-                rem_ref[group, e, :, 0:rem] = block[:, full * LANES :]
+                rem_ref[groups, e, :, 0:rem] = block[:, full * LANES :]
         if rem:
-            out[listed * full] = joined(group, listed).astype(out.dtype)
-
-    def take(pair):
+            out[listed * full] = joined(groups, listed).astype(out.dtype)
+
+    def take(pair, final):
         for sub in range(PAIR):
 
             def arrive(mask, carry, sub=sub):
-                arrival(mask, pair, sub).wait_recv()
+                arrival(mask, pair, sub, final).wait_recv()
                 return carry
 
             lax.fori_loop(1, groups, arrive, 0)
@@ -360,11 +413,11 @@
         for i in range(PAIR * base):
             scale_ref[pair * PAIR + i // base, i % base : i % base + 1, :] = rows[i]
 
-    def sent(pair):
+    def sent(pair, final):
         for sub in range(PAIR):
 
             def leave(mask, carry, sub=sub):
-                message(mask, pair, sub).wait_send()
+                message(mask, pair, sub, final).wait_send()
                 return carry
 
             lax.fori_loop(1, groups, leave, 0)
@@ -372,51 +425,66 @@
     def step(pair, carry):
         @pl.when(pair >= RING)
         def _():
-            sent(pair - RING)
+            sent(pair - RING, False)
 
         for sub in range(PAIR):
-            pack_layer(pair, sub)
+            prepare(pair, sub)
+            give(2, groups, pair, sub, False)
+            give(1, 2, pair, sub, False)
+            own(pair, sub, False)
 
         @pl.when(pair > 0)
         def _():
-            take(pair - 1)
+            take(pair - 1, False)
             unpack(pair - 1)
 
         return carry
 
     for ahead in range(1, parts_n):
         length_message(ahead).start()
-    lax.fori_loop(0, pairs, step, 0)
-
-    def give_list(mask, carry):
-        peer = partner(me, mask, groups)
-        pack_list(peer, 0, list_ref.at[0, peer])
-        list_message(mask).start()
-        return carry
-
-    lax.fori_loop(1, groups, give_list, 0)
-    pack_list(me, 0, first_ref.at[me])
-
-    def second(group, carry):
-        pack_list(group, 1, list_ref.at[1, group])
-        return carry
-
-    lax.fori_loop(0, groups, second, 0)
-    keep = pltpu.make_async_copy(list_ref.at[1], second_ref, second_sem)
-    keep.start()
-    for ahead in range(1, parts_n):
-        length_message(ahead).wait()
-        most = jnp.maximum(most, lengths_ref[ahead, 0:1, 0:1])
-    longest_ref[0, 0] = jnp.max(most).astype(jnp.int32)
-
-    take(pairs - 1)
-    unpack(pairs - 1)
-
-    def drain(pair, carry):
-        sent(pair)
-        return carry
-
-    lax.fori_loop(max(0, pairs - RING), pairs, drain, 0)
+    end = pairs - 1
+    lax.fori_loop(0, end, step, 0)
+
+    if end >= RING:
+        sent(end - RING, False)
+    for sub in range(PAIR - 1):
+        prepare(end, sub)
+        give(2, groups, end, sub, True)
+        give(1, 2, end, sub, True)
+        own(end, sub, True)
+    sub = PAIR - 1
+    early = max(2, groups * 3 // 4)
+    prepare(end, sub)
+    pack_list(lambda e: table_smem[layers + 1, e], all_ref.at[me])
+    for copy in stage(0):
+        list_message(*copy).start()
+    give(2, early, end, sub, True)
+    give(1, 2, end, sub, True)
+    own(end, sub, True)
+    take(end - 1, False)
+    unpack(end - 1)
+    for number in range(1, len(bits)):
+        for copy in stage(number - 1):
+            list_arrival(*copy).wait_recv()
+        for copy in stage(number):
+            list_message(*copy).start()
+        if number == 1:
+            give(early, groups, end, sub, True)
+
+            def second(group, carry):
+                for which in range(2):
+                    pack_list(
+                        lambda e: table_smem[layers, group * layers + which * listed + e], list_ref.at[group, which]
+                    )
+                return carry
+
+            lax.fori_loop(0, groups, second, 0)
+            keep = pltpu.make_async_copy(list_ref, second_ref, second_sem)
+            keep.start()
+            for ahead in range(1, parts_n):
+                length_message(ahead).wait()
+                most = jnp.maximum(most, lengths_ref[ahead, 0:1, :])
+            longest_ref[0, 0] = jnp.max(most).astype(jnp.int32)
 
     def edges(layer, carry):
         @pl.when(part < parts_n - 1)
@@ -431,23 +499,39 @@
 
     lax.fori_loop(0, layers, edges, 0)
     keep.wait()
-
-    def listed_all(mask, carry):
-        list_message(mask).wait()
+    for copy in stage(len(bits) - 1):
+        list_arrival(*copy).wait_recv()
+    for number in range(len(bits)):
+        for copy in stage(number):
+            list_message(*copy).wait_send()
+
+    def drain(pair, carry):
+        sent(pair, False)
         return carry
 
-    lax.fori_loop(1, groups, listed_all, 0)
-
-
-def list_places(group_ref, place_ref, slots):
+    lax.fori_loop(max(0, end - RING + 1), end, drain, 0)
+    sent(end, True)
+    take(end, True)
+
+
+def list_places(group_ref, place_ref, slots, groups, shared):
     layers = group_ref.shape[0]
     me = lax.axis_index("serve")
     count = jnp.sum(jnp.where(group_ref[...] == me, 1, 0), axis=1, keepdims=True)
+    ahead = jnp.zeros((layers, 1), jnp.int32)
+    every = jnp.where(count == slots, 1, 0)
+    if shared:
+        every = jnp.zeros((layers, 1), jnp.int32)
+        for g in range(groups):
+            filled = jnp.sum(jnp.where(group_ref[...] == g, 1, 0), axis=1, keepdims=True)
+            one = jnp.where(filled == slots, 1, 0)
+            ahead = ahead + jnp.where(g < me, one, 0)
+            every = every + one
     length = jnp.zeros((1, 1), jnp.int32)
     for n in range(layers):
-        long = count[n : n + 1, :] == slots
-        place_ref[n : n + 1, :] = jnp.broadcast_to(jnp.where(long, length, layers), (1, place_ref.shape[1]))
-        length = jnp.where(long, length + 1, length)
+        place = jnp.where(count[n : n + 1, :] == slots, length + ahead[n : n + 1, :], layers * groups)
+        place_ref[n : n + 1, :] = jnp.broadcast_to(place, (1, place_ref.shape[1]))
+        length = length + every[n : n + 1, :]
     return count
 
 
@@ -457,10 +541,13 @@
     group_ref,
     codes_ref,
     scale_ref,
-    first_ref,
+    tail_ref,
+    all_ref,
     codes_out,
     scale_out,
     scales,
+    codes,
+    rows,
     extra,
     extra_scale,
     rem_code,
@@ -472,20 +559,38 @@
     place_sem,
 ):
     full, rem, columns, groups = dims
-    layers = codes_ref.shape[0]
+    layers = scale_out.shape[0]
+    done = layers - PAIR
     listed = layers // 2
-    copies = [
-        pltpu.make_async_copy(codes_ref.at[n], codes_out.at[n, pl.ds(0, base)], sems.at[n]) for n in range(layers)
-    ]
+    copies = [pltpu.make_async_copy(codes_ref.at[n], codes_out.at[n, pl.ds(0, base)], sems.at[n]) for n in range(done)]
     for copy in copies:
         copy.start()
-    count = list_places(group_ref, place_ref, base + 1)
+    count = list_places(group_ref, place_ref, base + 1, groups, True)
     to_smem = pltpu.make_async_copy(place_ref, place_smem, place_sem)
     to_smem.start()
     extra[layers] = jnp.zeros(extra.shape[1:], extra.dtype)
+    scale_rest(dims, PAIR * base, lambda s, n: tail_ref[s, n], rem_code, rem_scale)
+
+    def last_pair(sub):
+        def slot(k, carry):
+            def put_code(low, high, code):
+                codes[sub, k, :, low:high] = code.astype(codes.dtype)
+
+            def put_scale(low, high, scale):
+                rows[sub * base + k, :, low:high] = scale
+
+            scale_slot(dims, sub * base + k, lambda s, n: tail_ref[s, n], rem_code, rem_scale, put_code, put_scale)
+            return carry
+
+        lax.fori_loop(0, base, slot, 0)
+        copies.append(pltpu.make_async_copy(codes.at[sub], codes_out.at[done + sub, pl.ds(0, base)], sems.at[done + sub]))
+        copies[-1].start()
+
+    for sub in range(PAIR):
+        last_pair(sub)
 
     def recv(s, n):
-        return first_ref[s, n]
+        return all_ref[s, n]
 
     scale_rest(dims, listed, recv, rem_code, rem_scale)
     slot = lax.broadcasted_iota(jnp.int32, scales.shape[1:], 0)
@@ -493,7 +598,7 @@
 
     def last_slot(layer, carry):
         place = place_smem[layer, 0]
-        long = place < layers
+        long = place < layers * groups
         extra_scale[layer] = jnp.zeros(extra_scale.shape[1:], jnp.float32)
 
         @pl.when(long)
@@ -512,9 +617,13 @@
         return carry
 
     lax.fori_loop(0, layers, last_slot, 0)
+    for sub in range(PAIR):
+        for k in range(base):
+            scales[done + sub, k : k + 1, :] = rows[sub * base + k]
     for n in range(layers):
-        own = jnp.where(slot < count[n : n + 1, :], scale_ref[n], 0.0)
-        scales[n] = jnp.where(slot < base, own, jnp.broadcast_to(extra_scale[n], own.shape))
+        scale = scale_ref[n] if n < done else scales[n]
+        scale = jnp.where(slot < count[n : n + 1, :], scale, 0.0)
+        scales[n] = jnp.where(slot < base, scale, jnp.broadcast_to(extra_scale[n], scale.shape))
     copies.append(pltpu.make_async_copy(scales, scale_out, sems.at[layers]))
     copies[-1].start()
     for n in range(layers):
@@ -545,37 +654,38 @@
     full, rem, columns, groups = dims
     layers = codes_out.shape[0]
     listed = layers // 2
-    list_places(group_ref, place_ref, base + 1)
+    list_places(group_ref, place_ref, base + 1, groups, False)
     to_smem = pltpu.make_async_copy(place_ref, place_smem, sem)
     to_smem.start()
     to_smem.wait()
-
-    def recv(s, n):
-        return got_ref[s, n]
-
-    scale_rest(dims, listed, recv, rem_code, rem_scale)
     slot = lax.broadcasted_iota(jnp.int32, scales.shape, 0)
-
-    def last_slot(layer, carry):
-        place = place_smem[layer, 0]
-
-        @pl.when((place >= listed) & (place < layers))
-        def _():
-            def put_code(low, high, code):
-                extra[:, low:high] = code.astype(extra.dtype)
-
-            def put_scale(low, high, scale):
-                extra_scale[:, low:high] = scale
-
-            scale_slot(dims, place - listed, recv, rem_code, rem_scale, put_code, put_scale)
-            pltpu.sync_copy(extra, codes_out.at[layer, base])
-            pltpu.sync_copy(scale_out.at[layer], scales)
-            scales[...] = jnp.where(slot < base, scales[...], jnp.broadcast_to(extra_scale[...], scales.shape))
-            pltpu.sync_copy(scales, scale_out.at[layer])
-
-        return carry
-
-    lax.fori_loop(0, layers, last_slot, 0)
+    for which in range(2):
+
+        def recv(s, n, which=which):
+            return got_ref[s, which, n]
+
+        scale_rest(dims, listed, recv, rem_code, rem_scale)
+
+        def last_slot(layer, carry, which=which, recv=recv):
+            place = place_smem[layer, 0] - which * listed
+
+            @pl.when((place >= 0) & (place < listed))
+            def _():
+                def put_code(low, high, code):
+                    extra[:, low:high] = code.astype(extra.dtype)
+
+                def put_scale(low, high, scale):
+                    extra_scale[:, low:high] = scale
+
+                scale_slot(dims, place, recv, rem_code, rem_scale, put_code, put_scale)
+                pltpu.sync_copy(extra, codes_out.at[layer, base])
+                pltpu.sync_copy(scale_out.at[layer], scales)
+                scales[...] = jnp.where(slot < base, scales[...], jnp.broadcast_to(extra_scale[...], scales.shape))
+                pltpu.sync_copy(scales, scale_out.at[layer])
+
+            return carry
+
+        lax.fori_loop(0, layers, last_slot, 0)
 
 
 def shards(train_weights, row_offset, block_group):
@@ -597,33 +707,35 @@
     dtype = train_weights.dtype
     dims = (full, rem, columns, serve_n)
     assert SHIFT == BLOCK and buffer_len % BLOCK == 0
-    assert rests * rem <= LANES and layers % PAIR == 0 and slots <= layers
+    assert rests * rem <= LANES and layers % PAIR == 0 and slots <= layers and pairs > 1
 
     group_ids = block_group[:, :, 0]
     smem = pl.BlockSpec(memory_space=pltpu.SMEM)
     vmem = pl.BlockSpec(memory_space=pltpu.VMEM)
     anywhere = pl.BlockSpec(memory_space=pl.ANY)
-    codes, scales, first, second, longest = pl.pallas_call(
+    hbm = pl.BlockSpec(memory_space=pltpu.HBM)
+    codes, scales, tail, shared, second, longest = pl.pallas_call(
         functools.partial(move_kernel, dims, base),
-        in_specs=[smem, vmem, anywhere],
-        out_specs=[vmem, vmem, vmem, pl.BlockSpec(memory_space=pltpu.HBM), smem],
+        in_specs=[anywhere, anywhere, anywhere],
+        out_specs=[vmem, vmem, vmem, vmem, hbm, smem],
         out_shape=[
-            pltpu.VMEM((layers, base, BLOCK, width), dtype),
-            pltpu.VMEM((layers, slots, width), jnp.float32),
+            pltpu.VMEM((layers - PAIR, base, BLOCK, width), dtype),
+            pltpu.VMEM((layers - PAIR, slots, width), jnp.float32),
+            pltpu.VMEM((serve_n, pieces, BLOCK, LANES), dtype),
             pltpu.VMEM((serve_n, pieces_list, BLOCK, LANES), dtype),
-            jax.ShapeDtypeStruct((serve_n, pieces_list, BLOCK, LANES), dtype),
+            jax.ShapeDtypeStruct((serve_n, 2, pieces_list, BLOCK, LANES), dtype),
             jax.ShapeDtypeStruct((1, 1), jnp.int32),
         ],
         scratch_shapes=[
-            pltpu.VMEM((serve_n, pairs, pieces, BLOCK, LANES), dtype),
+            pltpu.VMEM((serve_n, pairs - 1, pieces, BLOCK, LANES), dtype),
             pltpu.VMEM((serve_n, RING, pieces, BLOCK, LANES), dtype),
             pltpu.VMEM((PAIR, columns, buffer_len), dtype),
             pltpu.VMEM((buffer_len // BLOCK, BLOCK, columns), dtype),
-            pltpu.VMEM((serve_n, rests, BLOCK, LANES), dtype),
+            pltpu.VMEM((serve_n + 1, rests, BLOCK, LANES), dtype),
             pltpu.VMEM((layers, 2, SHIFT, columns), dtype),
             pltpu.VMEM((layers, 2, SHIFT, columns), dtype),
-            pltpu.VMEM((serve_n, layers + 1, BLOCK, columns), dtype),
-            pltpu.VMEM((2, serve_n, pieces_list, BLOCK, LANES), dtype),
+            pltpu.VMEM((serve_n * layers + 1, BLOCK, columns), dtype),
+            pltpu.VMEM((serve_n, 2, pieces_list, BLOCK, LANES), dtype),
             pltpu.VMEM((serve_n, BLOCK, LANES), jnp.float32),
             pltpu.VMEM((serve_n, 1, LANES), jnp.float32),
             pltpu.VMEM((PAIR * base, 1, width), jnp.float32),
@@ -631,14 +743,17 @@
             pltpu.SMEM((layers + 8, spots), jnp.int32),
             pltpu.VMEM((8, LANES), jnp.float32),
             pltpu.VMEM((train_n, 8, LANES), jnp.float32),
+            pltpu.SMEM((train_n + 1, layers), jnp.int32),
+            pltpu.VMEM((layers, blocks_dev), jnp.int32),
             pltpu.SemaphoreType.DMA((PAIR,)),
             pltpu.SemaphoreType.DMA,
+            pltpu.SemaphoreType.DMA((2,)),
             pltpu.SemaphoreType.DMA((serve_n, RING, PAIR)),
             pltpu.SemaphoreType.DMA((serve_n, pairs, PAIR)),
             pltpu.SemaphoreType.DMA((layers, 2)),
             pltpu.SemaphoreType.DMA((layers, 2)),
-            pltpu.SemaphoreType.DMA((serve_n,)),
-            pltpu.SemaphoreType.DMA((serve_n,)),
+            pltpu.SemaphoreType.DMA((2, serve_n)),
+            pltpu.SemaphoreType.DMA((2, serve_n)),
             pltpu.SemaphoreType.DMA((train_n,)),
             pltpu.SemaphoreType.DMA((train_n,)),
             pltpu.SemaphoreType.DMA,
@@ -651,7 +766,6 @@
 
     codes_shape = jax.ShapeDtypeStruct((layers, slots, BLOCK, width), dtype)
     scales_shape = jax.ShapeDtypeStruct((layers, slots, width), jnp.float32)
-    hbm = pl.BlockSpec(memory_space=pltpu.HBM)
     rest_scratch = [
         pltpu.VMEM((serve_n, BLOCK, LANES), jnp.float32),
         pltpu.VMEM((serve_n, 1, LANES), jnp.float32),
@@ -660,11 +774,13 @@
     ]
     codes_out, scales_out = pl.pallas_call(
         functools.partial(write_kernel, dims, base),
-        in_specs=[vmem, anywhere, vmem, vmem],
+        in_specs=[vmem, anywhere, vmem, vmem, vmem],
         out_specs=[hbm, hbm],
-        out_shape=[codes_shape, scales_shape],
+        out_shape=[codes_shape, pltpu.HBM((layers, slots, width), jnp.float32)],
         scratch_shapes=[
             pltpu.VMEM((layers, slots, width), jnp.float32),
+            pltpu.VMEM((PAIR, base, BLOCK, width), dtype),
+            pltpu.VMEM((PAIR * base, 1, width), jnp.float32),
             pltpu.VMEM((layers + 1, BLOCK, width), dtype),
             pltpu.VMEM((layers, 1, width), jnp.float32),
             *rest_scratch,
@@ -672,9 +788,9 @@
             pltpu.SemaphoreType.DMA((layers,)),
             pltpu.SemaphoreType.DMA,
         ],
-        compiler_params=pltpu.CompilerParams(vmem_limit_bytes=6 * MIB),
+        compiler_params=pltpu.CompilerParams(vmem_limit_bytes=10 * MIB),
         name="write",
-    )(group_ids, codes, scales, first)
+    )(group_ids, codes, scales, tail, shared)
 
     def late(state):
         got = lax.all_to_all(second, "serve", split_axis=0, concat_axis=0, tiled=True)

time: 198 us -> 189 us (0.955)
  Pallas kernels: 195 us -> 187 us
    pallas_call x1, Pallas kernels: 188 us -> 180 us  [shards(): pl.pallas_call(functools.partial(move_kernel, dims, base), in_specs=[anyw...]
where the time goes in v4:
time: 189 us
  Pallas kernels  187 us (99%)
    pallas_call x1, Pallas kernels, shards(): pl.pallas_call(functools.partial(move_kernel, dims, base), in_specs=[anyw...  180 us
    pallas_call x1, Pallas kernels, shards(): pl.pallas_call(functools.partial(write_kernel, dims, base), in_specs=[vme...  6.84 us

profile of v4, /device:TPU:1, one launch (start us, length us, event | category | flops | bytes accessed | tf_op | source)
XLA Modules:
  0.0 188.7 jit_solution(5332168354597725742)
XLA Ops:
  0.6 0.0 copy-start
  0.6 0.7 copy-done
  1.3 0.0 copy-start.3
  1.3 180.0 %move.1 = (bf16[14,7,32,2112]{3,2,1,0:T(8,128)(2,1)S(1)}, f32[14,8,2112]{2,1,0:T(8,128)S(1)}, bf16[8,29,32,128]{3,2,1,0:T(8,128)(2,1)S(1)}, bf16[8,17,32,128]{3,...) custom-call(s32[5,16]{1,0:T(8,128)S(1)} %bitcast.6, s32[16,56]{1,0:T(8,128)} %bitcast.10, ...), custom_call_target="tpu_custom_call" | custom-call | tf_op jit(solution)/shard_map/move/pallas_call | solution.py:717
  181.3 0.0 copy-done.3
  181.3 6.8 %write.1 = (bf16[16,8,32,2112]{3,2,1,0:T(8,128)(2,1)}, f32[16,8,2112]{2,1,0:T(8,128)}) custom-call(s32[16,56]{1,0:T(8,128)S(1)} %bitcast.11, bf16[14,7,32,2112]{3,2,1,0:T(8,128)(2,1)S(1)} %get-tuple-element.40.codes_ref, f32[14,8,2112]{2,1,0:T(8,128)S(1)} %get-tuple-element.41.scale_ref, bf16[8,29,32,128]{3,2,1,0:T(8,128)(2,1)S(1)} %get-tuple-element.42.tail_ref, ...), custom_call_target="tpu_custom_call" | custom-call | tf_op jit(solution)/shard_map/write/pallas_call | solution.py:775
  188.2 0.6 while.11
Async XLA Ops:
  0.6 0.7 copy-start
  1.3 180.0 %copy-start.3 = (s32[16,56,1]{1,2,0:T(1,128)S(1)}, s32[16,56,1]{1,2,0:T(1,128)}, u32[]{:S(2)}) copy-start(s32[16,56,1]{1,2,0:T(1,128)} %param.7) | copy-start | bytes 10756

commit v5 on v4

--- a/solution.py
+++ b/solution.py
@@ -12,6 +12,7 @@
 LANES = 128
 PAIR = 2
 RING = 3
+TURNS = 4
 MESH = pl.DeviceIdType.MESH
 MIB = 1024 * 1024
 
@@ -97,9 +98,11 @@
     codes_ref,
     scale_ref,
     tail_ref,
-    all_ref,
+    shared_codes,
+    shared_scale,
     second_ref,
     longest_ref,
+    all_ref,
     recv_ref,
     send_ref,
     in_ref,
@@ -155,7 +158,7 @@
             send_ref.at[peer, pair % RING, span],
             tail_ref.at[me, span] if final else recv_ref.at[me, pair, span],
             send_sem.at[mask, pair % RING, sub],
-            recv_sem.at[mask, pair, sub],
+            recv_sem.at[mask, pair % TURNS, sub],
             device_id={"serve": peer},
             device_id_type=MESH,
         )
@@ -168,18 +171,21 @@
             place,
             place,
             send_sem.at[mask, pair % RING, sub],
-            recv_sem.at[mask, pair, sub],
+            recv_sem.at[mask, pair % TURNS, sub],
             device_id={"serve": peer},
             device_id_type=MESH,
         )
 
     bits = [1 << n for n in range(groups.bit_length() - 1)]
-    orders = [bits[1:] + bits[:1], bits[:0:-1] + bits[:1]]
+    orders = [bits[1:], bits[:0:-1]]
     pieces_list = all_ref.shape[1]
     spans = [pl.ds(0, pieces_list // 2), pl.ds(pieces_list // 2, pieces_list - pieces_list // 2)]
 
     def stage(number):
         for which, order in enumerate(orders):
+            if number < 0:
+                yield which, 0, 0
+                continue
             held = [0]
             for bit in order[:number]:
                 held = held + [mask + bit for mask in held]
@@ -213,8 +219,8 @@
         return pltpu.make_async_remote_copy(
             edge_ref.at[layer, side],
             halo_ref.at[layer, side],
-            halo_send.at[layer, side],
-            halo_recv.at[layer, side],
+            halo_send.at[layer % 2, side],
+            halo_recv.at[layer % 2, side],
             device_id={"train": to},
             device_id_type=MESH,
         )
@@ -247,6 +253,174 @@
     for ahead in range(1, parts_n):
         pl.semaphore_signal(barrier, inc=1, device_id={"train": (part + ahead) % parts_n}, device_id_type=MESH)
 
+    row = lax.broadcasted_iota(jnp.int32, (BLOCK, columns), 0)
+    lane = lax.broadcasted_iota(jnp.int32, (BLOCK, LANES), 1)
+    last = rows_dev - BLOCK
+
+    def transpose_tile(sub, low):
+        high = min(low + LANES, buffer_len)
+        rows_of = turned(in_ref[sub, :, low:high]).astype(w_ref.dtype)
+        w_ref[low // BLOCK : high // BLOCK] = rows_of.reshape((high - low) // BLOCK, BLOCK, columns)
+
+    def joined(group, count):
+        tile = rem_ref[group, 0].astype(jnp.float32)
+        for i in range(1, count):
+            moved = pltpu.roll(rem_ref[group, i].astype(jnp.float32), i * rem, 1)
+            tile = jnp.where(lane >= i * rem, moved, tile)
+        return tile
+
+    def edge_ends(layer, act):
+        @pl.when(part < parts_n - 1)
+        def _():
+            act(edge(layer, 0))
+
+        @pl.when(part > 0)
+        def _():
+            act(edge(layer, 1))
+
+    def send_edges(layer, sub):
+        fetch(layer, sub).wait()
+        low = (buffer_len - 1) // LANES * LANES
+        edge_ref[layer, 0] = turned(in_ref[sub, :, low:buffer_len])[-SHIFT:].astype(edge_ref.dtype)
+        edge_ref[layer, 1] = turned(in_ref[sub, :, 0:LANES])[:SHIFT].astype(edge_ref.dtype)
+
+        @pl.when(layer >= 2)
+        def _():
+            edge_ends(layer - 2, lambda copy: copy.wait_send())
+
+        edge_ends(layer, lambda copy: copy.start())
+
+    def prepare(pair, sub):
+        layer = pair * PAIR + sub
+        for low in range(0, buffer_len, LANES):
+            transpose_tile(sub, low)
+
+        @pl.when(layer + PAIR < layers)
+        def _():
+            fetch(layer + PAIR, sub).start()
+
+        base_row = part * rows_dev
+
+        @pl.when(part > 0)
+        def _():
+            edge(layer, 0).wait_recv()
+            first = offset_ref[part, layer] - base_row
+            head = jnp.where(row < first, halo_ref[layer, 0].astype(jnp.float32), w_ref[1].astype(jnp.float32))
+            w_ref[1] = head.astype(w_ref.dtype)
+
+        @pl.when(part < parts_n - 1)
+        def _():
+            edge(layer, 1).wait_recv()
+            after = offset_ref[part + 1, layer] - base_row
+            tail = w_ref[blocks - 2].astype(jnp.float32)
+            tail = jnp.where(row + last >= after, halo_ref[layer, 1].astype(jnp.float32), tail)
+            w_ref[blocks - 2] = tail.astype(w_ref.dtype)
+
+        w_ref[0] = jnp.zeros((BLOCK, columns), w_ref.dtype)
+        if sub == 0:
+
+            @pl.when(pair == 0)
+            def _():
+                to_smem.wait()
+
+        def last_slots(group, carry):
+            over_ref[layer * groups + group] = w_ref[table_smem[layer, group * layers + base]]
+            return carry
+
+        lax.fori_loop(0, groups, last_slots, 0)
+
+    def gather(pair, sub, group, out):
+        for k in range(base):
+            block = w_ref[table_smem[pair * PAIR + sub, group * layers + k]]
+            for t in range(full):
+                out[(sub * base + k) * full + t] = block[:, t * LANES : (t + 1) * LANES]
+            if rem:
+                rem_ref[group, sub * base + k, :, 0:rem] = block[:, full * LANES :]
+        if rem and sub == PAIR - 1:
+            out[PAIR * half] = joined(group, PAIR * base).astype(out.dtype)
+
+    def give(low, high, pair, sub, final):
+        def one(mask, carry):
+            peer = partner(me, mask, groups)
+            gather(pair, sub, peer, send_ref.at[peer, pair % RING])
+            message(mask, pair, sub, final).start()
+            return carry
+
+        lax.fori_loop(low, high, one, 0)
+
+    def own(pair, sub, final):
+        gather(pair, sub, me, tail_ref.at[me] if final else recv_ref.at[me, pair])
+
+    def pack_list(entry_of, out):
+        for e in range(listed):
+            block = over_ref[entry_of(e)]
+            for t in range(full):
+                out[e * full + t] = block[:, t * LANES : (t + 1) * LANES]
+            if rem:
+                rem_ref[groups, e, :, 0:rem] = block[:, full * LANES :]
+        if rem:
+            out[listed * full] = joined(groups, listed).astype(out.dtype)
+
+    def take(pair, final):
+        for sub in range(PAIR):
+
+            def arrive(mask, carry, sub=sub):
+                arrival(mask, pair, sub, final).wait_recv()
+                return carry
+
+            lax.fori_loop(1, groups, arrive, 0)
+
+    def unpack(pair):
+        def recv(s, n):
+            return recv_ref[s, pair, n]
+
+        scale_rest(dims, PAIR * base, recv, rem_code, rem_scale)
+
+        def slot(i, carry):
+            def put_code(low, high, code):
+                codes_ref[pair * PAIR + i // base, i % base, :, low:high] = code.astype(codes_ref.dtype)
+
+            def put_scale(low, high, scale):
+                rows[i, :, low:high] = scale
+
+            scale_slot(dims, i, recv, rem_code, rem_scale, put_code, put_scale)
+            return carry
+
+        lax.fori_loop(0, PAIR * base, slot, 0)
+        for i in range(PAIR * base):
+            scale_ref[pair * PAIR + i // base, i % base : i % base + 1, :] = rows[i]
+
+    def sent(pair, final):
+        for sub in range(PAIR):
+
+            def leave(mask, carry, sub=sub):
+                message(mask, pair, sub, final).wait_send()
+                return carry
+
+            lax.fori_loop(1, groups, leave, 0)
+
+    def step(pair, carry):
+        @pl.when(pair >= RING)
+        def _():
+            sent(pair - RING, False)
+
+        for sub in range(PAIR):
+            prepare(pair, sub)
+            give(2, groups, pair, sub, False)
+            give(1, 2, pair, sub, False)
+            own(pair, sub, False)
+            send_edges(pair * PAIR + sub + 1, (sub + 1) % PAIR)
+
+        @pl.when(pair > 0)
+        def _():
+            take(pair - 1, False)
+            unpack(pair - 1)
+
+        return carry
+
+    pl.semaphore_wait(barrier, groups - 1 + parts_n - 1)
+    send_edges(0, 0)
+    get_offset.wait()
     get_group.wait()
     spot = lax.broadcasted_iota(jnp.int32, (layers, groups * layers), 1)
     spot_group = jnp.zeros(spot.shape, jnp.int32)
@@ -282,163 +456,6 @@
     most = total.astype(jnp.float32)
     length_ref[...] = jnp.broadcast_to(most, length_ref.shape)
     over_ref[none] = jnp.zeros((BLOCK, columns), over_ref.dtype)
-    get_offset.wait()
-    to_smem.wait()
-    pl.semaphore_wait(barrier, groups - 1 + parts_n - 1)
-
-    row = lax.broadcasted_iota(jnp.int32, (BLOCK, columns), 0)
-    lane = lax.broadcasted_iota(jnp.int32, (BLOCK, LANES), 1)
-    last = rows_dev - BLOCK
-
-    def transpose_tile(sub, low):
-        high = min(low + LANES, buffer_len)
-        rows_of = turned(in_ref[sub, :, low:high]).astype(w_ref.dtype)
-        w_ref[low // BLOCK : high // BLOCK] = rows_of.reshape((high - low) // BLOCK, BLOCK, columns)
-
-    def joined(group, count):
-        tile = rem_ref[group, 0].astype(jnp.float32)
-        for i in range(1, count):
-            moved = pltpu.roll(rem_ref[group, i].astype(jnp.float32), i * rem, 1)
-            tile = jnp.where(lane >= i * rem, moved, tile)
-        return tile
-
-    def prepare(pair, sub):
-        layer = pair * PAIR + sub
-        fetch(layer, sub).wait()
-        lows = list(range(0, buffer_len, LANES))
-        lows = [lows[0], lows[-1]] + lows[1:-1]
-        for low in lows[:2]:
-            transpose_tile(sub, low)
-        edge_ref[layer, 0] = w_ref[blocks - 1]
-        edge_ref[layer, 1] = w_ref[0]
-
-        @pl.when(part < parts_n - 1)
-        def _():
-            edge(layer, 0).start()
-
-        @pl.when(part > 0)
-        def _():
-            edge(layer, 1).start()
-
-        for low in lows[2:]:
-            transpose_tile(sub, low)
-
-        @pl.when(layer + PAIR < layers)
-        def _():
-            fetch(layer + PAIR, sub).start()
-
-        base_row = part * rows_dev
-
-        @pl.when(part > 0)
-        def _():
-            edge(layer, 0).wait_recv()
-            first = offset_ref[part, layer] - base_row
-            head = jnp.where(row < first, halo_ref[layer, 0].astype(jnp.float32), w_ref[1].astype(jnp.float32))
-            w_ref[1] = head.astype(w_ref.dtype)
-
-        @pl.when(part < parts_n - 1)
-        def _():
-            edge(layer, 1).wait_recv()
-            after = offset_ref[part + 1, layer] - base_row
-            tail = w_ref[blocks - 2].astype(jnp.float32)
-            tail = jnp.where(row + last >= after, halo_ref[layer, 1].astype(jnp.float32), tail)
-            w_ref[blocks - 2] = tail.astype(w_ref.dtype)
-
-        w_ref[0] = jnp.zeros((BLOCK, columns), w_ref.dtype)
-
-        def last_slots(group, carry):
-            over_ref[layer * groups + group] = w_ref[table_smem[layer, group * layers + base]]
-            return carry
-
-        lax.fori_loop(0, groups, last_slots, 0)
-
-    def gather(pair, sub, group, out):
-        for k in range(base):
-            block = w_ref[table_smem[pair * PAIR + sub, group * layers + k]]
-            for t in range(full):
-                out[(sub * base + k) * full + t] = block[:, t * LANES : (t + 1) * LANES]
-            if rem:
-                rem_ref[group, sub * base + k, :, 0:rem] = block[:, full * LANES :]
-        if rem and sub == PAIR - 1:
-            out[PAIR * half] = joined(group, PAIR * base).astype(out.dtype)
-
-    def give(low, high, pair, sub, final):
-        def one(mask, carry):
-            peer = partner(me, mask, groups)
-            gather(pair, sub, peer, send_ref.at[peer, pair % RING])
-            message(mask, pair, sub, final).start()
-            return carry
-
-        lax.fori_loop(low, high, one, 0)
-
-    def own(pair, sub, final):
-        gather(pair, sub, me, tail_ref.at[me] if final else recv_ref.at[me, pair])
-
-    def pack_list(entry_of, out):
-        for e in range(listed):
-            block = over_ref[entry_of(e)]
-            for t in range(full):
-                out[e * full + t] = block[:, t * LANES : (t + 1) * LANES]
-            if rem:
-                rem_ref[groups, e, :, 0:rem] = block[:, full * LANES :]
-        if rem:
-            out[listed * full] = joined(groups, listed).astype(out.dtype)
-
-    def take(pair, final):
-        for sub in range(PAIR):
-
-            def arrive(mask, carry, sub=sub):
-                arrival(mask, pair, sub, final).wait_recv()
-                return carry
-
-            lax.fori_loop(1, groups, arrive, 0)
-
-    def unpack(pair):
-        def recv(s, n):
-            return recv_ref[s, pair, n]
-
-        scale_rest(dims, PAIR * base, recv, rem_code, rem_scale)
-
-        def slot(i, carry):
-            def put_code(low, high, code):
-                codes_ref[pair * PAIR + i // base, i % base, :, low:high] = code.astype(codes_ref.dtype)
-
-            def put_scale(low, high, scale):
-                rows[i, :, low:high] = scale
-
-            scale_slot(dims, i, recv, rem_code, rem_scale, put_code, put_scale)
-            return carry
-
-        lax.fori_loop(0, PAIR * base, slot, 0)
-        for i in range(PAIR * base):
-            scale_ref[pair * PAIR + i // base, i % base : i % base + 1, :] = rows[i]
-
-    def sent(pair, final):
-        for sub in range(PAIR):
-
-            def leave(mask, carry, sub=sub):
-                message(mask, pair, sub, final).wait_send()
-                return carry
-
-            lax.fori_loop(1, groups, leave, 0)
-
-    def step(pair, carry):
-        @pl.when(pair >= RING)
-        def _():
-            sent(pair - RING, False)
-
-        for sub in range(PAIR):
-            prepare(pair, sub)
-            give(2, groups, pair, sub, False)
-            give(1, 2, pair, sub, False)
-            own(pair, sub, False)
-
-        @pl.when(pair > 0)
-        def _():
-            take(pair - 1, False)
-            unpack(pair - 1)
-
-        return carry
 
     for ahead in range(1, parts_n):
         length_message(ahead).start()
@@ -452,56 +469,75 @@
         give(2, groups, end, sub, True)
         give(1, 2, end, sub, True)
         own(end, sub, True)
+        send_edges(end * PAIR + sub + 1, sub + 1)
     sub = PAIR - 1
-    early = max(2, groups * 3 // 4)
+    direct = max(2, groups * 3 // 4)
     prepare(end, sub)
     pack_list(lambda e: table_smem[layers + 1, e], all_ref.at[me])
     for copy in stage(0):
         list_message(*copy).start()
-    give(2, early, end, sub, True)
+    for which in range(2):
+        list_message(which, 1, 0).start()
+    give(direct, groups, end, sub, True)
     give(1, 2, end, sub, True)
     own(end, sub, True)
+
+    def second(group, carry):
+        for which in range(2):
+            pack_list(lambda e: table_smem[layers, group * layers + which * listed + e], list_ref.at[group, which])
+        return carry
+
+    lax.fori_loop(0, groups, second, 0)
+    keep = pltpu.make_async_copy(list_ref, second_ref, second_sem)
+    keep.start()
+    for ahead in range(1, parts_n):
+        length_message(ahead).wait()
+        most = jnp.maximum(most, lengths_ref[ahead, 0:1, :])
+    longest_ref[0, 0] = jnp.max(most).astype(jnp.int32)
+    for n in range(2):
+        edge_ends(layers - 1 - n, lambda copy: copy.wait_send())
+
     take(end - 1, False)
     unpack(end - 1)
-    for number in range(1, len(bits)):
+    high = len(bits) - 1
+    for number in range(1, high + 1):
         for copy in stage(number - 1):
             list_arrival(*copy).wait_recv()
-        for copy in stage(number):
-            list_message(*copy).start()
+        if number < high:
+            for copy in stage(number):
+                list_message(*copy).start()
+        for which, bit, mask in stage(number - 1):
+            list_message(which, 1, bit + mask).start()
         if number == 1:
-            give(early, groups, end, sub, True)
-
-            def second(group, carry):
-                for which in range(2):
-                    pack_list(
-                        lambda e: table_smem[layers, group * layers + which * listed + e], list_ref.at[group, which]
-                    )
-                return carry
-
-            lax.fori_loop(0, groups, second, 0)
-            keep = pltpu.make_async_copy(list_ref, second_ref, second_sem)
-            keep.start()
-            for ahead in range(1, parts_n):
-                length_message(ahead).wait()
-                most = jnp.maximum(most, lengths_ref[ahead, 0:1, :])
-            longest_ref[0, 0] = jnp.max(most).astype(jnp.int32)
-
-    def edges(layer, carry):
-        @pl.when(part < parts_n - 1)
-        def _():
-            edge(layer, 0).wait_send()
-
-        @pl.when(part > 0)
-        def _():
-            edge(layer, 1).wait_send()
-
+            give(2, direct, end, sub, True)
+    if high < 1:
+        give(2, direct, end, sub, True)
+    for which, bit, mask in [copy for number in range(-1, high) for copy in stage(number)]:
+        list_arrival(which, 1, bit + mask).wait_recv()
+
+    def recv(s, n):
+        return all_ref[s, n]
+
+    scale_rest(dims, listed, recv, rem_code, rem_scale)
+
+    def listed_slot(e, carry):
+        def put_code(low, high, code):
+            shared_codes[e, :, low:high] = code.astype(shared_codes.dtype)
+
+        def put_scale(low, high, scale):
+            shared_scale[e, :, low:high] = scale
+
+        scale_slot(dims, e, recv, rem_code, rem_scale, put_code, put_scale)
         return carry
 
-    lax.fori_loop(0, layers, edges, 0)
+    lax.fori_loop(0, listed, listed_slot, 0)
+    shared_codes[listed] = jnp.zeros(shared_codes.shape[1:], shared_codes.dtype)
+    shared_scale[listed] = jnp.zeros(shared_scale.shape[1:], jnp.float32)
+
     keep.wait()
-    for copy in stage(len(bits) - 1):
-        list_arrival(*copy).wait_recv()
-    for number in range(len(bits)):
+    for which, bit, mask in [copy for number in range(-1, high) for copy in stage(number)]:
+        list_message(which, 1, bit + mask).wait_send()
+    for number in range(high):
         for copy in stage(number):
             list_message(*copy).wait_send()
 
@@ -542,23 +578,22 @@
     codes_ref,
     scale_ref,
     tail_ref,
-    all_ref,
+    shared_codes,
+    shared_scale,
     codes_out,
     scale_out,
     scales,
     codes,
     rows,
-    extra,
-    extra_scale,
     rem_code,
     rem_scale,
     place_ref,
     place_smem,
     sems,
-    extra_sems,
+    last_sems,
     place_sem,
 ):
-    full, rem, columns, groups = dims
+    groups = dims[3]
     layers = scale_out.shape[0]
     done = layers - PAIR
     listed = layers // 2
@@ -568,8 +603,11 @@
     count = list_places(group_ref, place_ref, base + 1, groups, True)
     to_smem = pltpu.make_async_copy(place_ref, place_smem, place_sem)
     to_smem.start()
-    extra[layers] = jnp.zeros(extra.shape[1:], extra.dtype)
-    scale_rest(dims, PAIR * base, lambda s, n: tail_ref[s, n], rem_code, rem_scale)
+
+    def recv(s, n):
+        return tail_ref[s, n]
+
+    scale_rest(dims, PAIR * base, recv, rem_code, rem_scale)
 
     def last_pair(sub):
         def slot(k, carry):
@@ -579,55 +617,31 @@
             def put_scale(low, high, scale):
                 rows[sub * base + k, :, low:high] = scale
 
-            scale_slot(dims, sub * base + k, lambda s, n: tail_ref[s, n], rem_code, rem_scale, put_code, put_scale)
+            scale_slot(dims, sub * base + k, recv, rem_code, rem_scale, put_code, put_scale)
             return carry
 
         lax.fori_loop(0, base, slot, 0)
         copies.append(pltpu.make_async_copy(codes.at[sub], codes_out.at[done + sub, pl.ds(0, base)], sems.at[done + sub]))
         copies[-1].start()
 
-    for sub in range(PAIR):
+    last_pair(0)
+    to_smem.wait()
+    places = [jnp.minimum(place_smem[n, 0], listed) for n in range(layers)]
+    for n in range(layers):
+        copies.append(pltpu.make_async_copy(shared_codes.at[places[n]], codes_out.at[n, base], last_sems.at[n]))
+        copies[-1].start()
+    for sub in range(1, PAIR):
         last_pair(sub)
-
-    def recv(s, n):
-        return all_ref[s, n]
-
-    scale_rest(dims, listed, recv, rem_code, rem_scale)
     slot = lax.broadcasted_iota(jnp.int32, scales.shape[1:], 0)
-    to_smem.wait()
-
-    def last_slot(layer, carry):
-        place = place_smem[layer, 0]
-        long = place < layers * groups
-        extra_scale[layer] = jnp.zeros(extra_scale.shape[1:], jnp.float32)
-
-        @pl.when(long)
-        def _():
-            def put_code(low, high, code):
-                extra[layer, :, low:high] = code.astype(extra.dtype)
-
-            def put_scale(low, high, scale):
-                extra_scale[layer, :, low:high] = scale
-
-            scale_slot(dims, jnp.minimum(place, listed - 1), recv, rem_code, rem_scale, put_code, put_scale)
-
-        pltpu.make_async_copy(
-            extra.at[jnp.where(long, layer, layers)], codes_out.at[layer, base], extra_sems.at[layer]
-        ).start()
-        return carry
-
-    lax.fori_loop(0, layers, last_slot, 0)
     for sub in range(PAIR):
         for k in range(base):
             scales[done + sub, k : k + 1, :] = rows[sub * base + k]
     for n in range(layers):
         scale = scale_ref[n] if n < done else scales[n]
         scale = jnp.where(slot < count[n : n + 1, :], scale, 0.0)
-        scales[n] = jnp.where(slot < base, scale, jnp.broadcast_to(extra_scale[n], scale.shape))
+        scales[n] = jnp.where(slot < base, scale, jnp.broadcast_to(shared_scale[places[n]], scale.shape))
     copies.append(pltpu.make_async_copy(scales, scale_out, sems.at[layers]))
     copies[-1].start()
-    for n in range(layers):
-        copies.append(pltpu.make_async_copy(extra.at[n], codes_out.at[n, base], extra_sems.at[n]))
     for copy in copies:
         copy.wait()
 
@@ -714,19 +728,21 @@
     vmem = pl.BlockSpec(memory_space=pltpu.VMEM)
     anywhere = pl.BlockSpec(memory_space=pl.ANY)
     hbm = pl.BlockSpec(memory_space=pltpu.HBM)
-    codes, scales, tail, shared, second, longest = pl.pallas_call(
+    codes, scales, tail, shared_codes, shared_scale, second, longest = pl.pallas_call(
         functools.partial(move_kernel, dims, base),
-        in_specs=[anywhere, anywhere, anywhere],
-        out_specs=[vmem, vmem, vmem, vmem, hbm, smem],
+        in_specs=[hbm, hbm, hbm],
+        out_specs=[vmem, vmem, vmem, vmem, vmem, hbm, smem],
         out_shape=[
             pltpu.VMEM((layers - PAIR, base, BLOCK, width), dtype),
             pltpu.VMEM((layers - PAIR, slots, width), jnp.float32),
             pltpu.VMEM((serve_n, pieces, BLOCK, LANES), dtype),
-            pltpu.VMEM((serve_n, pieces_list, BLOCK, LANES), dtype),
+            pltpu.VMEM((listed + 1, BLOCK, width), dtype),
+            pltpu.VMEM((listed + 1, 1, width), jnp.float32),
             jax.ShapeDtypeStruct((serve_n, 2, pieces_list, BLOCK, LANES), dtype),
             jax.ShapeDtypeStruct((1, 1), jnp.int32),
         ],
         scratch_shapes=[
+            pltpu.VMEM((serve_n, pieces_list, BLOCK, LANES), dtype),
             pltpu.VMEM((serve_n, pairs - 1, pieces, BLOCK, LANES), dtype),
             pltpu.VMEM((serve_n, RING, pieces, BLOCK, LANES), dtype),
             pltpu.VMEM((PAIR, columns, buffer_len), dtype),
@@ -749,9 +765,9 @@
             pltpu.SemaphoreType.DMA,
             pltpu.SemaphoreType.DMA((2,)),
             pltpu.SemaphoreType.DMA((serve_n, RING, PAIR)),
-            pltpu.SemaphoreType.DMA((serve_n, pairs, PAIR)),
-            pltpu.SemaphoreType.DMA((layers, 2)),
-            pltpu.SemaphoreType.DMA((layers, 2)),
+            pltpu.SemaphoreType.DMA((serve_n, TURNS, PAIR)),
+            pltpu.SemaphoreType.DMA((2, 2)),
+            pltpu.SemaphoreType.DMA((2, 2)),
             pltpu.SemaphoreType.DMA((2, serve_n)),
             pltpu.SemaphoreType.DMA((2, serve_n)),
             pltpu.SemaphoreType.DMA((train_n,)),
@@ -774,15 +790,13 @@
     ]
     codes_out, scales_out = pl.pallas_call(
         functools.partial(write_kernel, dims, base),
-        in_specs=[vmem, anywhere, vmem, vmem, vmem],
+        in_specs=[vmem, anywhere, vmem, vmem, vmem, vmem],
         out_specs=[hbm, hbm],
         out_shape=[codes_shape, pltpu.HBM((layers, slots, width), jnp.float32)],
         scratch_shapes=[
             pltpu.VMEM((layers, slots, width), jnp.float32),
             pltpu.VMEM((PAIR, base, BLOCK, width), dtype),
             pltpu.VMEM((PAIR * base, 1, width), jnp.float32),
-            pltpu.VMEM((layers + 1, BLOCK, width), dtype),
-            pltpu.VMEM((layers, 1, width), jnp.float32),
             *rest_scratch,
             pltpu.SemaphoreType.DMA((layers + 1,)),
             pltpu.SemaphoreType.DMA((layers,)),
@@ -790,7 +804,7 @@
         ],
         compiler_params=pltpu.CompilerParams(vmem_limit_bytes=10 * MIB),
         name="write",
-    )(group_ids, codes, scales, tail, shared)
+    )(group_ids, codes, scales, tail, shared_codes, shared_scale)
 
     def late(state):
         got = lax.all_to_all(second, "serve", split_axis=0, concat_axis=0, tiled=True)

time: 189 us -> 188 us (level)
  no operation moved by 1% of the time
where the time goes in v5:
time: 188 us; the launch traced here: 187 us
  Pallas kernels  186 us (99%)
    pallas_call x1, Pallas kernels, shards(): pl.pallas_call(functools.partial(move_kernel, dims, base), in_specs=[hbm,...  179 us
    pallas_call x1, Pallas kernels, shards(): pl.pallas_call(functools.partial(write_kernel, dims, base), in_specs=[vme...  6.82 us

profile of v5, /device:TPU:1, one launch (start us, length us, event | category | flops | bytes accessed | tf_op | source)
XLA Modules:
  0.0 187.5 jit_solution(882370417682871376)
XLA Ops:
  0.6 0.0 copy-start
  0.6 0.7 copy-done
  1.3 0.0 copy-start.3
  1.3 178.8 %move.1 = (bf16[14,7,32,2112]{3,2,1,0:T(8,128)(2,1)S(1)}, f32[14,8,2112]{2,1,0:T(8,128)S(1)}, bf16[8,29,32,128]{3,2,1,0:T(8,128)(2,1)S(1)}, bf16[9,32,2112]{2,1,...) custom-call(s32[5,16]{1,0:T(8,128)S(1)} %bitcast.6, ...), custom_call_target="tpu_custom_call" | custom-call | tf_op jit(solution)/shard_map/move/pallas_call | solution.py:731
  180.1 0.0 copy-done.3
  180.1 6.8 %write.1 = (bf16[16,8,32,2112]{3,2,1,0:T(8,128)(2,1)}, f32[16,8,2112]{2,1,0:T(8,128)}) custom-call(s32[16,56]{1,0:T(8,128)S(1)} %bitcast.11, bf16[14,7,32,2112]{3,2,1,0:T(8,128)(2,1)S(1)} %get-tuple-element.41.codes_ref, f32[14,8,2112]{2,1,0:T(8,128)S(1)} %get-tuple-element.42.scale_ref, bf16[8,29,32,128]{3,2,1,0:T(8,128)(2,1)S(1)} %get-tuple-element.43.tail_ref, ...), custom_call_target="tpu_custom_call" | custom-call | tf_op jit(solution)/shard_map/write/pallas_call | solution.py:791
  186.9 0.6 while.11
Async XLA Ops:
  0.6 0.7 copy-start
  1.3 178.8 %copy-start.3 = (s32[16,56,1]{1,2,0:T(1,128)S(1)}, s32[16,56,1]{1,2,0:T(1,128)}, u32[]{:S(2)}) copy-start(s32[16,56,1]{1,2,0:T(1,128)} %param.7) | copy-start | bytes 10756

commit v6 on v5

--- a/solution.py
+++ b/solution.py
@@ -119,6 +119,7 @@
     table_smem,
     length_ref,
     lengths_ref,
+    longest_smem,
     offset_ref,
     group_ref,
     in_sem,
@@ -157,24 +158,22 @@
         return pltpu.make_async_remote_copy(
             send_ref.at[peer, pair % RING, span],
             tail_ref.at[me, span] if final else recv_ref.at[me, pair, span],
-            send_sem.at[mask, pair % RING, sub],
-            recv_sem.at[mask, pair % TURNS, sub],
+            send_sem.at[pair % RING, sub],
+            recv_sem.at[pair % TURNS, sub],
             device_id={"serve": peer},
             device_id_type=MESH,
         )
 
-    def arrival(mask, pair, sub, final):
-        peer = partner(me, mask, groups)
+    def arrival(pair, sub, final):
         span = pl.ds(sub * half, rest if sub == PAIR - 1 else half)
-        place = tail_ref.at[peer, span] if final else recv_ref.at[peer, pair, span]
-        return pltpu.make_async_remote_copy(
-            place,
-            place,
-            send_sem.at[mask, pair % RING, sub],
-            recv_sem.at[mask, pair % TURNS, sub],
-            device_id={"serve": peer},
-            device_id_type=MESH,
-        )
+        others = pl.ds(0, groups - 1)
+        place = tail_ref.at[others, span] if final else recv_ref.at[others, pair, span]
+        return pltpu.make_async_copy(place, place, recv_sem.at[pair % TURNS, sub])
+
+    def departure(pair, sub):
+        span = pl.ds(sub * half, rest if sub == PAIR - 1 else half)
+        place = send_ref.at[pl.ds(0, groups - 1), pair % RING, span]
+        return pltpu.make_async_copy(place, place, send_sem.at[pair % RING, sub])
 
     bits = [1 << n for n in range(groups.bit_length() - 1)]
     orders = [bits[1:], bits[:0:-1]]
@@ -192,27 +191,20 @@
             for mask in held:
                 yield which, order[number], mask
 
-    def list_message(which, bit, mask):
+    def list_message(number, which, bit, mask):
         place = all_ref.at[partner(me, mask, groups), spans[which]]
         return pltpu.make_async_remote_copy(
             place,
             place,
-            list_send.at[which, bit + mask],
-            list_recv.at[which, bit + mask],
+            list_send.at[number],
+            list_recv.at[number],
             device_id={"serve": partner(me, bit, groups)},
             device_id_type=MESH,
         )
 
-    def list_arrival(which, bit, mask):
-        place = all_ref.at[partner(me, bit + mask, groups), spans[which]]
-        return pltpu.make_async_remote_copy(
-            place,
-            place,
-            list_send.at[which, bit + mask],
-            list_recv.at[which, bit + mask],
-            device_id={"serve": partner(me, bit, groups)},
-            device_id_type=MESH,
-        )
+    def lists_passed(number, sem):
+        place = all_ref.at[pl.ds(0, 1 << number)]
+        return pltpu.make_async_copy(place, place, sem.at[number])
 
     def edge(layer, side):
         to = part + 1 if side == 0 else part - 1
@@ -225,16 +217,17 @@
             device_id_type=MESH,
         )
 
-    def length_message(ahead):
+    def length_message(turn, side):
         return pltpu.make_async_remote_copy(
-            length_ref,
-            lengths_ref.at[ahead],
-            length_send.at[ahead],
-            length_recv.at[ahead],
-            device_id={"train": (part + ahead) % parts_n},
+            length_ref.at[turn],
+            lengths_ref.at[turn, side],
+            length_send.at[side],
+            length_recv.at[turn, side],
+            device_id={"train": part + 1 if side == 0 else part - 1},
             device_id_type=MESH,
         )
 
+    lengths_ref[...] = jnp.zeros(lengths_ref.shape, jnp.float32)
     get_group = pltpu.make_async_copy(group_hbm, group_ref, small_sem.at[0])
     get_group.start()
     fetch(0, 0).start()
@@ -250,8 +243,17 @@
         return carry
 
     lax.fori_loop(1, groups, greet, 0)
-    for ahead in range(1, parts_n):
-        pl.semaphore_signal(barrier, inc=1, device_id={"train": (part + ahead) % parts_n}, device_id_type=MESH)
+
+    @pl.when(part > 0)
+    def _():
+        pl.semaphore_signal(barrier, inc=1, device_id={"train": part - 1}, device_id_type=MESH)
+
+    @pl.when(part < parts_n - 1)
+    def _():
+        pl.semaphore_signal(barrier, inc=1, device_id={"train": part + 1}, device_id_type=MESH)
+
+    below = (part + parts_n - 1) // parts_n
+    above = (2 * parts_n - 2 - part) // parts_n
 
     row = lax.broadcasted_iota(jnp.int32, (BLOCK, columns), 0)
     lane = lax.broadcasted_iota(jnp.int32, (BLOCK, LANES), 1)
@@ -339,11 +341,13 @@
         if rem and sub == PAIR - 1:
             out[PAIR * half] = joined(group, PAIR * base).astype(out.dtype)
 
-    def give(low, high, pair, sub, final):
+    def give(low, high, pair, sub, pack, send, final):
         def one(mask, carry):
             peer = partner(me, mask, groups)
-            gather(pair, sub, peer, send_ref.at[peer, pair % RING])
-            message(mask, pair, sub, final).start()
+            if pack:
+                gather(pair, sub, peer, send_ref.at[peer, pair % RING])
+            if send:
+                message(mask, pair, sub, final).start()
             return carry
 
         lax.fori_loop(low, high, one, 0)
@@ -363,12 +367,7 @@
 
     def take(pair, final):
         for sub in range(PAIR):
-
-            def arrive(mask, carry, sub=sub):
-                arrival(mask, pair, sub, final).wait_recv()
-                return carry
-
-            lax.fori_loop(1, groups, arrive, 0)
+            arrival(pair, sub, final).wait()
 
     def unpack(pair):
         def recv(s, n):
@@ -390,24 +389,19 @@
         for i in range(PAIR * base):
             scale_ref[pair * PAIR + i // base, i % base : i % base + 1, :] = rows[i]
 
-    def sent(pair, final):
+    def sent(pair):
         for sub in range(PAIR):
-
-            def leave(mask, carry, sub=sub):
-                message(mask, pair, sub, final).wait_send()
-                return carry
-
-            lax.fori_loop(1, groups, leave, 0)
+            departure(pair, sub).wait()
 
     def step(pair, carry):
         @pl.when(pair >= RING)
         def _():
-            sent(pair - RING, False)
+            sent(pair - RING)
 
         for sub in range(PAIR):
             prepare(pair, sub)
-            give(2, groups, pair, sub, False)
-            give(1, 2, pair, sub, False)
+            give(2, groups, pair, sub, True, True, False)
+            give(1, 2, pair, sub, True, True, False)
             own(pair, sub, False)
             send_edges(pair * PAIR + sub + 1, (sub + 1) % PAIR)
 
@@ -418,7 +412,7 @@
 
         return carry
 
-    pl.semaphore_wait(barrier, groups - 1 + parts_n - 1)
+    pl.semaphore_wait(barrier, groups - 1 + below + above)
     send_edges(0, 0)
     get_offset.wait()
     get_group.wait()
@@ -453,34 +447,29 @@
     table_ref[layers + 1 : layers + 2, 0:LANES] = shared
     to_smem = pltpu.make_async_copy(table_ref, table_smem, table_sem)
     to_smem.start()
-    most = total.astype(jnp.float32)
-    length_ref[...] = jnp.broadcast_to(most, length_ref.shape)
+    most = jnp.broadcast_to(total.astype(jnp.float32), length_ref.shape[1:])
     over_ref[none] = jnp.zeros((BLOCK, columns), over_ref.dtype)
 
-    for ahead in range(1, parts_n):
-        length_message(ahead).start()
     end = pairs - 1
     lax.fori_loop(0, end, step, 0)
 
     if end >= RING:
-        sent(end - RING, False)
+        sent(end - RING)
+    for sub in range(PAIR):
+        prepare(end, sub)
+        give(1, groups, end, sub, True, False, True)
+        own(end, sub, True)
+        if sub < PAIR - 1:
+            send_edges(end * PAIR + sub + 1, sub + 1)
+    pack_list(lambda e: table_smem[layers + 1, e], all_ref.at[me])
+    high = len(bits) - 1
+    for copy in stage(0):
+        list_message(0, *copy).start()
+    for which in range(2):
+        list_message(high, which, 1, 0).start()
     for sub in range(PAIR - 1):
-        prepare(end, sub)
-        give(2, groups, end, sub, True)
-        give(1, 2, end, sub, True)
-        own(end, sub, True)
-        send_edges(end * PAIR + sub + 1, sub + 1)
-    sub = PAIR - 1
-    direct = max(2, groups * 3 // 4)
-    prepare(end, sub)
-    pack_list(lambda e: table_smem[layers + 1, e], all_ref.at[me])
-    for copy in stage(0):
-        list_message(*copy).start()
-    for which in range(2):
-        list_message(which, 1, 0).start()
-    give(direct, groups, end, sub, True)
-    give(1, 2, end, sub, True)
-    own(end, sub, True)
+        give(2, groups, end, sub, False, True, True)
+        give(1, 2, end, sub, False, True, True)
 
     def second(group, carry):
         for which in range(2):
@@ -488,32 +477,53 @@
         return carry
 
     lax.fori_loop(0, groups, second, 0)
-    keep = pltpu.make_async_copy(list_ref, second_ref, second_sem)
+    keep = pltpu.make_async_copy(list_ref, second_ref, second_sem.at[0])
     keep.start()
-    for ahead in range(1, parts_n):
-        length_message(ahead).wait()
-        most = jnp.maximum(most, lengths_ref[ahead, 0:1, :])
-    longest_ref[0, 0] = jnp.max(most).astype(jnp.int32)
     for n in range(2):
         edge_ends(layers - 1 - n, lambda copy: copy.wait_send())
 
+    def to_neighbours(turn, act):
+        @pl.when(part < parts_n - 1)
+        def _():
+            act(length_message(turn, 0))
+
+        @pl.when(part > 0)
+        def _():
+            act(length_message(turn, 1))
+
+    def from_neighbours(turn):
+        @pl.when(part > 0)
+        def _():
+            length_message(turn, 0).wait_recv()
+
+        @pl.when(part < parts_n - 1)
+        def _():
+            length_message(turn, 1).wait_recv()
+
+    for turn in range(parts_n - 1):
+        length_ref[turn] = most
+        to_neighbours(turn, lambda copy: copy.start())
+        from_neighbours(turn)
+        for side in range(2):
+            most = jnp.maximum(most, lengths_ref[turn, side])
+        to_neighbours(turn, lambda copy: copy.wait_send())
+    longest_smem[0, 0] = jnp.max(most).astype(jnp.int32)
+    tell = pltpu.make_async_copy(longest_smem, longest_ref, second_sem.at[1])
+    tell.start()
+
     take(end - 1, False)
     unpack(end - 1)
-    high = len(bits) - 1
     for number in range(1, high + 1):
-        for copy in stage(number - 1):
-            list_arrival(*copy).wait_recv()
+        lists_passed(number - 1, list_recv).wait()
         if number < high:
             for copy in stage(number):
-                list_message(*copy).start()
+                list_message(number, *copy).start()
         for which, bit, mask in stage(number - 1):
-            list_message(which, 1, bit + mask).start()
+            list_message(high, which, 1, bit + mask).start()
         if number == 1:
-            give(2, direct, end, sub, True)
-    if high < 1:
-        give(2, direct, end, sub, True)
-    for which, bit, mask in [copy for number in range(-1, high) for copy in stage(number)]:
-        list_arrival(which, 1, bit + mask).wait_recv()
+            give(groups * 3 // 4, groups, end, PAIR - 1, False, True, True)
+            give(1, groups * 3 // 4, end, PAIR - 1, False, True, True)
+    lists_passed(high, list_recv).wait()
 
     def recv(s, n):
         return all_ref[s, n]
@@ -535,18 +545,11 @@
     shared_scale[listed] = jnp.zeros(shared_scale.shape[1:], jnp.float32)
 
     keep.wait()
-    for which, bit, mask in [copy for number in range(-1, high) for copy in stage(number)]:
-        list_message(which, 1, bit + mask).wait_send()
-    for number in range(high):
-        for copy in stage(number):
-            list_message(*copy).wait_send()
-
-    def drain(pair, carry):
-        sent(pair, False)
-        return carry
-
-    lax.fori_loop(max(0, end - RING + 1), end, drain, 0)
-    sent(end, True)
+    tell.wait()
+    for number in range(high + 1):
+        lists_passed(number, list_send).wait()
+    for pair in range(max(0, end - RING + 1), end + 1):
+        sent(pair)
     take(end, True)
 
 
@@ -731,7 +734,7 @@
     codes, scales, tail, shared_codes, shared_scale, second, longest = pl.pallas_call(
         functools.partial(move_kernel, dims, base),
         in_specs=[hbm, hbm, hbm],
-        out_specs=[vmem, vmem, vmem, vmem, vmem, hbm, smem],
+        out_specs=[vmem, vmem, vmem, vmem, vmem, hbm, hbm],
         out_shape=[
             pltpu.VMEM((layers - PAIR, base, BLOCK, width), dtype),
             pltpu.VMEM((layers - PAIR, slots, width), jnp.float32),
@@ -757,28 +760,29 @@
             pltpu.VMEM((PAIR * base, 1, width), jnp.float32),
             pltpu.VMEM((layers + 8, spots), jnp.int32),
             pltpu.SMEM((layers + 8, spots), jnp.int32),
-            pltpu.VMEM((8, LANES), jnp.float32),
             pltpu.VMEM((train_n, 8, LANES), jnp.float32),
+            pltpu.VMEM((train_n, 2, 8, LANES), jnp.float32),
+            pltpu.SMEM((1, 1), jnp.int32),
             pltpu.SMEM((train_n + 1, layers), jnp.int32),
             pltpu.VMEM((layers, blocks_dev), jnp.int32),
             pltpu.SemaphoreType.DMA((PAIR,)),
             pltpu.SemaphoreType.DMA,
             pltpu.SemaphoreType.DMA((2,)),
-            pltpu.SemaphoreType.DMA((serve_n, RING, PAIR)),
-            pltpu.SemaphoreType.DMA((serve_n, TURNS, PAIR)),
+            pltpu.SemaphoreType.DMA((RING, PAIR)),
+            pltpu.SemaphoreType.DMA((TURNS, PAIR)),
             pltpu.SemaphoreType.DMA((2, 2)),
             pltpu.SemaphoreType.DMA((2, 2)),
-            pltpu.SemaphoreType.DMA((2, serve_n)),
-            pltpu.SemaphoreType.DMA((2, serve_n)),
-            pltpu.SemaphoreType.DMA((train_n,)),
-            pltpu.SemaphoreType.DMA((train_n,)),
-            pltpu.SemaphoreType.DMA,
+            pltpu.SemaphoreType.DMA((serve_n.bit_length() - 1,)),
+            pltpu.SemaphoreType.DMA((serve_n.bit_length() - 1,)),
+            pltpu.SemaphoreType.DMA((2,)),
+            pltpu.SemaphoreType.DMA((train_n, 2)),
+            pltpu.SemaphoreType.DMA((2,)),
         ],
         compiler_params=pltpu.CompilerParams(
             collective_id=0, has_side_effects=True, vmem_limit_bytes=36 * MIB
         ),
         name="move",
-    )(row_offset.T, group_ids, jnp.swapaxes(train_weights, 1, 2))
+    )(pltpu.with_memory_space_constraint(row_offset.T, pltpu.HBM), group_ids, jnp.swapaxes(train_weights, 1, 2))
 
     codes_shape = jax.ShapeDtypeStruct((layers, slots, BLOCK, width), dtype)
     scales_shape = jax.ShapeDtypeStruct((layers, slots, width), jnp.float32)

time: 188 us -> 185 us (0.984)
  Pallas kernels: 186 us -> 183 us
    pallas_call x1, Pallas kernels: 179 us -> 176 us  [shards(): pl.pallas_call(functools.partial(move_kernel, dims, base), in_specs=[hbm,...]
where the time goes in v6:
time: 185 us
  Pallas kernels  183 us (99%)
    pallas_call x1, Pallas kernels, shards(): pl.pallas_call(functools.partial(move_kernel, dims, base), in_specs=[hbm,...  176 us
    pallas_call x1, Pallas kernels, shards(): pl.pallas_call(functools.partial(write_kernel, dims, base), in_specs=[vme...  6.82 us

profile of v6, /device:TPU:1, one launch (start us, length us, event | category | flops | bytes accessed | tf_op | source)
XLA Modules:
  0.0 184.5 jit_solution(14997600412517728946)
XLA Ops:
  0.6 0.0 copy-start.2
  0.6 176.3 %move.1 = (bf16[14,7,32,2112]{3,2,1,0:T(8,128)(2,1)S(1)}, f32[14,8,2112]{2,1,0:T(8,128)S(1)}, bf16[8,29,32,128]{3,2,1,0:T(8,128)(2,1)S(1)}, bf16[9,32,2112]{2,1,...) custom-call(s32[5,16]{1,0:T(8,128)} %bitcast.12, ...), custom_call_target="tpu_custom_call" | custom-call | tf_op jit(solution)/shard_map/move/pallas_call | solution.py:734
  177.0 0.0 copy-done.2
  177.0 6.8 %write.1 = (bf16[16,8,32,2112]{3,2,1,0:T(8,128)(2,1)}, f32[16,8,2112]{2,1,0:T(8,128)}) custom-call(s32[16,56]{1,0:T(8,128)S(1)} %bitcast.10, bf16[14,7,32,2112]{3,2,1,0:T(8,128)(2,1)S(1)} %get-tuple-element.41.codes_ref, f32[14,8,2112]{2,1,0:T(8,128)S(1)} %get-tuple-element.42.scale_ref, bf16[8,29,32,128]{3,2,1,0:T(8,128)(2,1)S(1)} %get-tuple-element.43.tail_ref, ...), custom_call_target="tpu_custom_call" | custom-call | tf_op jit(solution)/shard_map/write/pallas_call | solution.py:795
  183.8 0.7 while.11
Async XLA Ops:
  0.6 176.4 %copy-start.2 = (s32[16,56,1]{1,2,0:T(1,128)S(1)}, s32[16,56,1]{1,2,0:T(1,128)}, u32[]{:S(2)}) copy-start(s32[16,56,1]{1,2,0:T(1,128)} %param.7) | copy-start | bytes 10756

commit v7 on v6

--- a/solution.py
+++ b/solution.py
@@ -42,7 +42,8 @@
             rem_code[s], rem_scale[s] = scaled(recv(s, count * full))
 
 
-def scale_slot(dims, i, recv, rem_code, rem_scale, put_code, put_scale):
+def scale_slot(dims, i, recv, rem_code, rem_scale, put_code, put_scale, place=None):
+    place = i if place is None else place
     full, rem, columns, sources = dims
     width = columns * sources
     tiles = -(-width // LANES)
@@ -79,7 +80,7 @@
                 if low:
                     code, scale = pltpu.roll(code, low, 1), pltpu.roll(scale, low, 1)
             else:
-                turn = lax.rem(low + LANES - i * rem, LANES)
+                turn = lax.rem(low + LANES - place * rem, LANES)
                 code, scale = pltpu.roll(rem_code[s], turn, 1), pltpu.roll(rem_scale[s], turn, 1)
             tile = start // LANES
             put(tile, low, code, scale)
@@ -103,6 +104,7 @@
     second_ref,
     longest_ref,
     all_ref,
+    turned_ref,
     recv_ref,
     send_ref,
     in_ref,
@@ -148,16 +150,24 @@
     parts_n = lax.axis_size("train")
     half = base * full
     rest = half + (1 if rem else 0)
+    ahead = base > 2
 
     def fetch(layer, sub):
         return pltpu.make_async_copy(wt_ref.at[layer], in_ref.at[sub], in_sem.at[sub])
 
-    def message(mask, pair, sub, final):
+    def landing(source, pair, sub, final):
+        if ahead and isinstance(pair, int) and pair == 0 and sub == 0:
+            return turned_ref.at[source]
+        return tail_ref.at[source] if final else recv_ref.at[source, pair]
+
+    def message(mask, pair, sub, final, slots_of=None):
         peer = partner(me, mask, groups)
         span = pl.ds(sub * half, rest if sub == PAIR - 1 else half)
+        if slots_of is not None:
+            span = pl.ds(slots_of[0] * full, (slots_of[1] - slots_of[0]) * full)
         return pltpu.make_async_remote_copy(
             send_ref.at[peer, pair % RING, span],
-            tail_ref.at[me, span] if final else recv_ref.at[me, pair, span],
+            landing(me, pair, sub, final).at[span],
             send_sem.at[pair % RING, sub],
             recv_sem.at[pair % TURNS, sub],
             device_id={"serve": peer},
@@ -292,7 +302,7 @@
 
         edge_ends(layer, lambda copy: copy.start())
 
-    def prepare(pair, sub):
+    def turn_layer(pair, sub):
         layer = pair * PAIR + sub
         for low in range(0, buffer_len, LANES):
             transpose_tile(sub, low)
@@ -301,6 +311,10 @@
         def _():
             fetch(layer + PAIR, sub).start()
 
+        w_ref[0] = jnp.zeros((BLOCK, columns), w_ref.dtype)
+
+    def finish_layer(pair, sub):
+        layer = pair * PAIR + sub
         base_row = part * rows_dev
 
         @pl.when(part > 0)
@@ -318,21 +332,18 @@
             tail = jnp.where(row + last >= after, halo_ref[layer, 1].astype(jnp.float32), tail)
             w_ref[blocks - 2] = tail.astype(w_ref.dtype)
 
-        w_ref[0] = jnp.zeros((BLOCK, columns), w_ref.dtype)
-        if sub == 0:
-
-            @pl.when(pair == 0)
-            def _():
-                to_smem.wait()
-
         def last_slots(group, carry):
             over_ref[layer * groups + group] = w_ref[table_smem[layer, group * layers + base]]
             return carry
 
         lax.fori_loop(0, groups, last_slots, 0)
 
-    def gather(pair, sub, group, out):
-        for k in range(base):
+    def prepare(pair, sub):
+        turn_layer(pair, sub)
+        finish_layer(pair, sub)
+
+    def gather(pair, sub, group, out, slots_of=None):
+        for k in range(*(slots_of or (0, base))):
             block = w_ref[table_smem[pair * PAIR + sub, group * layers + k]]
             for t in range(full):
                 out[(sub * base + k) * full + t] = block[:, t * LANES : (t + 1) * LANES]
@@ -341,19 +352,19 @@
         if rem and sub == PAIR - 1:
             out[PAIR * half] = joined(group, PAIR * base).astype(out.dtype)
 
-    def give(low, high, pair, sub, pack, send, final):
+    def give(low, high, pair, sub, pack, send, final, slots_of=None):
         def one(mask, carry):
             peer = partner(me, mask, groups)
             if pack:
-                gather(pair, sub, peer, send_ref.at[peer, pair % RING])
+                gather(pair, sub, peer, send_ref.at[peer, pair % RING], slots_of)
             if send:
-                message(mask, pair, sub, final).start()
+                message(mask, pair, sub, final, slots_of).start()
             return carry
 
         lax.fori_loop(low, high, one, 0)
 
     def own(pair, sub, final):
-        gather(pair, sub, me, tail_ref.at[me] if final else recv_ref.at[me, pair])
+        gather(pair, sub, me, landing(me, pair, sub, final))
 
     def pack_list(entry_of, out):
         for e in range(listed):
@@ -382,7 +393,11 @@
             def put_scale(low, high, scale):
                 rows[i, :, low:high] = scale
 
-            scale_slot(dims, i, recv, rem_code, rem_scale, put_code, put_scale)
+            place = i
+            if ahead:
+                place = table_smem[layers + 2, me * layers + jnp.minimum(i, base - 1)]
+                place = jnp.where((pair == 0) & (i < base), place, i)
+            scale_slot(dims, i, recv, rem_code, rem_scale, put_code, put_scale, place)
             return carry
 
         lax.fori_loop(0, PAIR * base, slot, 0)
@@ -405,16 +420,23 @@
             own(pair, sub, False)
             send_edges(pair * PAIR + sub + 1, (sub + 1) % PAIR)
 
-        @pl.when(pair > 0)
-        def _():
-            take(pair - 1, False)
-            unpack(pair - 1)
-
+        take(pair - 1, False)
+        if ahead:
+
+            @pl.when(pair == 1)
+            def _():
+                def restore(source, inner):
+                    for k in range(base):
+                        place = table_smem[layers + 2, me * layers + k]
+                        for t in range(full):
+                            recv_ref[source, 0, k * full + t] = turned_ref[source, place * full + t]
+                    return inner
+
+                lax.fori_loop(0, groups, restore, 0)
+
+        unpack(pair - 1)
         return carry
 
-    pl.semaphore_wait(barrier, groups - 1 + below + above)
-    send_edges(0, 0)
-    get_offset.wait()
     get_group.wait()
     spot = lax.broadcasted_iota(jnp.int32, (layers, groups * layers), 1)
     spot_group = jnp.zeros(spot.shape, jnp.int32)
@@ -423,11 +445,21 @@
     spot_slot = spot - spot_group * layers
     seen = jnp.zeros(spot.shape, jnp.int32)
     table = jnp.zeros(spot.shape, jnp.int32)
+    moved = jnp.zeros((1, groups * layers), jnp.int32)
     for j in range(group_ref.shape[1]):
         mine = group_ref[:, j : j + 1] == spot_group
         table = jnp.where(mine & (seen == spot_slot), j + 1, table)
+        moved = jnp.where(mine[0:1, :] & (seen[0:1, :] + 1 == spot_slot[0:1, :]), j + 1, moved)
         seen = jnp.where(mine, seen + 1, seen)
     table_ref[0:layers, :] = table
+    if ahead:
+        count, k = seen[0:1, :], spot_slot[0:1, :]
+        final_block = group_ref.shape[1]
+        turns = (group_ref[0:1, final_block - 1 : final_block] == spot_group[0:1, :]) & (count <= base)
+        turned_row = jnp.where(k == 0, final_block, jnp.where(k < count, moved, 0))
+        table_ref[0:1, :] = jnp.where(turns, turned_row, table[0:1, :])
+        position = jnp.where(k == count - 1, 0, jnp.where(k < count, k + 1, k))
+        table_ref[layers + 2 : layers + 3, :] = jnp.where(turns, position, k)
     none = layers * groups
     length = jnp.zeros((1, groups * layers), jnp.int32)
     entry = jnp.full(length.shape, none, jnp.int32)
@@ -450,8 +482,25 @@
     most = jnp.broadcast_to(total.astype(jnp.float32), length_ref.shape[1:])
     over_ref[none] = jnp.zeros((BLOCK, columns), over_ref.dtype)
 
+    pl.semaphore_wait(barrier, groups - 1 + below + above)
+    send_edges(0, 0)
+    get_offset.wait()
     end = pairs - 1
-    lax.fori_loop(0, end, step, 0)
+    to_smem.wait()
+    for sub in range(PAIR):
+        turn_layer(0, sub)
+        if sub == 0 and ahead:
+            give(2, groups, 0, sub, True, True, False, (2, base))
+            finish_layer(0, sub)
+            give(2, groups, 0, sub, True, True, False, (0, 2))
+            give(1, 2, 0, sub, True, True, False)
+        else:
+            finish_layer(0, sub)
+            give(2, groups, 0, sub, True, True, False)
+            give(1, 2, 0, sub, True, True, False)
+        own(0, sub, False)
+        send_edges(sub + 1, (sub + 1) % PAIR)
+    lax.fori_loop(1, end, step, 0)
 
     if end >= RING:
         sent(end - RING)
@@ -724,7 +773,7 @@
     dtype = train_weights.dtype
     dims = (full, rem, columns, serve_n)
     assert SHIFT == BLOCK and buffer_len % BLOCK == 0
-    assert rests * rem <= LANES and layers % PAIR == 0 and slots <= layers and pairs > 1
+    assert rests * rem <= LANES and layers % PAIR == 0 and slots <= layers and pairs > 2
 
     group_ids = block_group[:, :, 0]
     smem = pl.BlockSpec(memory_space=pltpu.SMEM)
@@ -746,6 +795,7 @@
         ],
         scratch_shapes=[
             pltpu.VMEM((serve_n, pieces_list, BLOCK, LANES), dtype),
+            pltpu.VMEM((serve_n, base * full, BLOCK, LANES), dtype),
             pltpu.VMEM((serve_n, pairs - 1, pieces, BLOCK, LANES), dtype),
             pltpu.VMEM((serve_n, RING, pieces, BLOCK, LANES), dtype),
             pltpu.VMEM((PAIR, columns, buffer_len), dtype),

time: 185 us -> 183 us (0.989)
  Pallas kernels: 183 us -> 181 us
    pallas_call x1, Pallas kernels: 176 us -> 174 us  [shards(): pl.pallas_call(functools.partial(move_kernel, dims, base), in_specs=[hbm,...]
where the time goes in v7:
time: 183 us; the launch traced here: 182 us
  Pallas kernels  181 us (99%)
    pallas_call x1, Pallas kernels, shards(): pl.pallas_call(functools.partial(move_kernel, dims, base), in_specs=[hbm,...  174 us
    pallas_call x1, Pallas kernels, shards(): pl.pallas_call(functools.partial(write_kernel, dims, base), in_specs=[vme...  6.82 us

profile of v7, /device:TPU:1, one launch (start us, length us, event | category | flops | bytes accessed | tf_op | source)
XLA Modules:
  0.0 182.4 jit_solution(12512951276919750849)
XLA Ops:
  0.6 0.0 copy-start.2
  0.6 174.2 %move.1 = (bf16[14,7,32,2112]{3,2,1,0:T(8,128)(2,1)S(1)}, f32[14,8,2112]{2,1,0:T(8,128)S(1)}, bf16[8,29,32,128]{3,2,1,0:T(8,128)(2,1)S(1)}, bf16[9,32,2112]{2,1,...) custom-call(s32[5,16]{1,0:T(8,128)} %bitcast.12, ...), custom_call_target="tpu_custom_call" | custom-call | tf_op jit(solution)/shard_map/move/pallas_call | solution.py:783
  174.9 0.0 copy-done.2
  174.9 6.8 %write.1 = (bf16[16,8,32,2112]{3,2,1,0:T(8,128)(2,1)}, f32[16,8,2112]{2,1,0:T(8,128)}) custom-call(s32[16,56]{1,0:T(8,128)S(1)} %bitcast.10, bf16[14,7,32,2112]{3,2,1,0:T(8,128)(2,1)S(1)} %get-tuple-element.41.codes_ref, f32[14,8,2112]{2,1,0:T(8,128)S(1)} %get-tuple-element.42.scale_ref, bf16[8,29,32,128]{3,2,1,0:T(8,128)(2,1)S(1)} %get-tuple-element.43.tail_ref, ...), custom_call_target="tpu_custom_call" | custom-call | tf_op jit(solution)/shard_map/write/pallas_call | solution.py:845
  181.7 0.7 while.11
Async XLA Ops:
  0.6 174.2 %copy-start.2 = (s32[16,56,1]{1,2,0:T(1,128)S(1)}, s32[16,56,1]{1,2,0:T(1,128)}, u32[]{:S(2)}) copy-start(s32[16,56,1]{1,2,0:T(1,128)} %param.7) | copy-start | bytes 10756

commit v8 on v7

--- a/solution.py
+++ b/solution.py
@@ -238,6 +238,22 @@
         )
 
     lengths_ref[...] = jnp.zeros(lengths_ref.shape, jnp.float32)
+    barrier = pltpu.get_barrier_semaphore()
+
+    def greet(mask, carry):
+        pl.semaphore_signal(barrier, inc=1, device_id={"serve": partner(me, mask, groups)}, device_id_type=MESH)
+        return carry
+
+    lax.fori_loop(1, groups, greet, 0)
+
+    @pl.when(part > 0)
+    def _():
+        pl.semaphore_signal(barrier, inc=1, device_id={"train": part - 1}, device_id_type=MESH)
+
+    @pl.when(part < parts_n - 1)
+    def _():
+        pl.semaphore_signal(barrier, inc=1, device_id={"train": part + 1}, device_id_type=MESH)
+
     get_group = pltpu.make_async_copy(group_hbm, group_ref, small_sem.at[0])
     get_group.start()
     fetch(0, 0).start()
@@ -246,22 +262,6 @@
     for sub in range(1, PAIR):
         fetch(sub, sub).start()
 
-    barrier = pltpu.get_barrier_semaphore()
-
-    def greet(mask, carry):
-        pl.semaphore_signal(barrier, inc=1, device_id={"serve": partner(me, mask, groups)}, device_id_type=MESH)
-        return carry
-
-    lax.fori_loop(1, groups, greet, 0)
-
-    @pl.when(part > 0)
-    def _():
-        pl.semaphore_signal(barrier, inc=1, device_id={"train": part - 1}, device_id_type=MESH)
-
-    @pl.when(part < parts_n - 1)
-    def _():
-        pl.semaphore_signal(barrier, inc=1, device_id={"train": part + 1}, device_id_type=MESH)
-
     below = (part + parts_n - 1) // parts_n
     above = (2 * parts_n - 2 - part) // parts_n
 
@@ -290,11 +290,15 @@
         def _():
             act(edge(layer, 1))
 
-    def send_edges(layer, sub):
+    def store_edges(layer, sub):
         fetch(layer, sub).wait()
         low = (buffer_len - 1) // LANES * LANES
         edge_ref[layer, 0] = turned(in_ref[sub, :, low:buffer_len])[-SHIFT:].astype(edge_ref.dtype)
         edge_ref[layer, 1] = turned(in_ref[sub, :, 0:LANES])[:SHIFT].astype(edge_ref.dtype)
+
+
+    def send_edges(layer, sub):
+        store_edges(layer, sub)
 
         @pl.when(layer >= 2)
         def _():
@@ -482,13 +486,16 @@
     most = jnp.broadcast_to(total.astype(jnp.float32), length_ref.shape[1:])
     over_ref[none] = jnp.zeros((BLOCK, columns), over_ref.dtype)
 
+    end = pairs - 1
+    store_edges(0, 0)
+    turn_layer(0, 0)
+    to_smem.wait()
     pl.semaphore_wait(barrier, groups - 1 + below + above)
-    send_edges(0, 0)
+    edge_ends(0, lambda copy: copy.start())
     get_offset.wait()
-    end = pairs - 1
-    to_smem.wait()
     for sub in range(PAIR):
-        turn_layer(0, sub)
+        if sub > 0:
+            turn_layer(0, sub)
         if sub == 0 and ahead:
             give(2, groups, 0, sub, True, True, False, (2, base))
             finish_layer(0, sub)

time: 183 us -> 182 us (level)
  no operation moved by 1% of the time
where the time goes in v8:
time: 182 us
  Pallas kernels  181 us (99%)
    pallas_call x1, Pallas kernels, shards(): pl.pallas_call(functools.partial(move_kernel, dims, base), in_specs=[hbm,...  174 us
    pallas_call x1, Pallas kernels, shards(): pl.pallas_call(functools.partial(write_kernel, dims, base), in_specs=[vme...  6.82 us

profile of v8, /device:TPU:1, one launch (start us, length us, event | category | flops | bytes accessed | tf_op | source)
XLA Modules:
  0.0 182.0 jit_solution(246716951929127809)
XLA Ops:
  0.6 0.0 copy-start.2
  0.6 173.8 %move.1 = (bf16[14,7,32,2112]{3,2,1,0:T(8,128)(2,1)S(1)}, f32[14,8,2112]{2,1,0:T(8,128)S(1)}, bf16[8,29,32,128]{3,2,1,0:T(8,128)(2,1)S(1)}, bf16[9,32,2112]{2,1,...) custom-call(s32[5,16]{1,0:T(8,128)} %bitcast.12, ...), custom_call_target="tpu_custom_call" | custom-call | tf_op jit(solution)/shard_map/move/pallas_call | solution.py:790
  174.5 0.0 copy-done.2
  174.5 6.8 %write.1 = (bf16[16,8,32,2112]{3,2,1,0:T(8,128)(2,1)}, f32[16,8,2112]{2,1,0:T(8,128)}) custom-call(s32[16,56]{1,0:T(8,128)S(1)} %bitcast.10, bf16[14,7,32,2112]{3,2,1,0:T(8,128)(2,1)S(1)} %get-tuple-element.41.codes_ref, f32[14,8,2112]{2,1,0:T(8,128)S(1)} %get-tuple-element.42.scale_ref, bf16[8,29,32,128]{3,2,1,0:T(8,128)(2,1)S(1)} %get-tuple-element.43.tail_ref, ...), custom_call_target="tpu_custom_call" | custom-call | tf_op jit(solution)/shard_map/write/pallas_call | solution.py:852
  181.3 0.7 while.11
Async XLA Ops:
  0.6 173.8 %copy-start.2 = (s32[16,56,1]{1,2,0:T(1,128)S(1)}, s32[16,56,1]{1,2,0:T(1,128)}, u32[]{:S(2)}) copy-start(s32[16,56,1]{1,2,0:T(1,128)} %param.7) | copy-start | bytes 10756

commit v9 on v8

--- a/solution.py
+++ b/solution.py
@@ -887,8 +887,9 @@
         )(group_ids, got, state[1], state[2])
         return jnp.zeros((), jnp.int32), late_codes, late_scales
 
-    state = (longest[0, 0], codes_out, scales_out)
-    _, codes_out, scales_out = lax.while_loop(lambda now: now[0] > listed, late, state)
+    codes_out, scales_out = lax.cond(
+        longest[0, 0] > listed, lambda c, z: late((0, c, z))[1:], lambda c, z: (c, z), codes_out, scales_out
+    )
     return (
         codes_out.reshape(layers, 1, 1, slots, BLOCK, width),
         scales_out.reshape(layers, 1, 1, slots, width),

time: 182 us -> 182 us (level)
  no operation moved by 1% of the time
where the time goes in v9:
time: 182 us
  Pallas kernels  181 us (99%)
    pallas_call x1, Pallas kernels, shards(): pl.pallas_call(functools.partial(move_kernel, dims, base), in_specs=[hbm,...  174 us
    pallas_call x1, Pallas kernels, shards(): pl.pallas_call(functools.partial(write_kernel, dims, base), in_specs=[vme...  6.82 us

profile of v9, /device:TPU:1, one launch (start us, length us, event | category | flops | bytes accessed | tf_op | source)
XLA Modules:
  0.0 182.0 jit_solution(12289819358919597445)
XLA Ops:
  0.6 0.0 copy-start.2
  0.6 173.8 %move.1 = (bf16[14,7,32,2112]{3,2,1,0:T(8,128)(2,1)S(1)}, f32[14,8,2112]{2,1,0:T(8,128)S(1)}, bf16[8,29,32,128]{3,2,1,0:T(8,128)(2,1)S(1)}, bf16[9,32,2112]{2,1,...) custom-call(s32[5,16]{1,0:T(8,128)} %bitcast.16, ...), custom_call_target="tpu_custom_call" | custom-call | tf_op jit(solution)/shard_map/move/pallas_call | solution.py:790
  175.1 0.0 copy-done.2
  175.2 6.8 %write.1 = (bf16[16,8,32,2112]{3,2,1,0:T(8,128)(2,1)}, f32[16,8,2112]{2,1,0:T(8,128)}) custom-call(s32[16,56]{1,0:T(8,128)S(1)} %bitcast.14, bf16[14,7,32,2112]{3,2,1,0:T(8,128)(2,1)S(1)} %get-tuple-element.38.codes_ref, f32[14,8,2112]{2,1,0:T(8,128)S(1)} %get-tuple-element.39.scale_ref, bf16[8,29,32,128]{3,2,1,0:T(8,128)(2,1)S(1)} %get-tuple-element.40.tail_ref, ...), custom_call_target="tpu_custom_call" | custom-call | tf_op jit(solution)/shard_map/write/pallas_call | solution.py:852
  (1 shorter events, 0.0 us)
Async XLA Ops:
  0.6 174.5 %copy-start.2 = (s32[16,56,1]{1,2,0:T(1,128)S(1)}, s32[16,56,1]{1,2,0:T(1,128)}, u32[]{:S(2)}) copy-start(s32[16,56,1]{1,2,0:T(1,128)} %param.7) | copy-start | bytes 10756
